TPU v7x, 32 devices: a whole 2x2x4 slice. The times are simulated.
32 devices in a mesh: cell: 8 (over z, y), inst: 4 (over x, core).
Axes of the slice: x: 2, y: 2, z: 4, core: 2. Of those that a mesh axis runs over, the one named last changes fastest.
Arguments:
- fine_residual: float32 [8, 6, 65536], P('inst', None, 'cell'), may hold values from -6 to 6
- fine_map: int32 [65536], P('cell'), may hold values from 0 to 15
- routes: int32 [8, 64], P('cell'), may hold values from 0 to 7, as said below
- receive_lists: int32 [8, 192], P('cell'), may hold values from 0 to 1023
- neighbours: int32 [6, 8192], P(None, 'cell'), may hold values from 0 to 1215, as said below
- face_weights: float32 [6, 8192], P(None, 'cell'), may hold values from 0.3 to 3
- spectral_coef: float32 [8192], P('cell'), may hold values from 0.2 to 1
- diag_extra: float32 [6, 8192], P(None, 'cell'), may hold values from 0.5 to 2
Outputs:
- fine_correction: float32 [8, 6, 65536], P('inst', None, 'cell')
- coarse_correction: float32 [8, 6, 8192], P('inst', None, 'cell')
Inputs may be any that keep to these rules, and one draw needn't show every extreme that they name: `routes`: in row p, the value p appears 64 - 2 * 4 times, and (p - 1) mod 8 and (p + 1) mod 8 appear 4 times each. `receive_lists`: row o, entries t * 32 to t * 32 + 31, list cells that partition o receives as halo from partition (o + d) mod 8, with d = t - 3 for t < 3 and d = t - 2 otherwise. `neighbours`: A value below 1024 is a cell of the own partition; a value x of 1024 or more is halo slot x - 1024.
All inputs are finite; a program needn't handle non-finite values.
Results may differ from a plain program's by a relative error of at most 0.0001.
Values sent between devices are 32-bit elements; how exact they have to be, the bound alone decides.
No kernel may reach another device: no remote copies, remote signals or barrier semaphores. Data moves between devices by JAX's collectives and lax.ppermute only.
A program may use at most 64 MiB of HBM per device.

v0:
```python
import jax
import jax.numpy as jnp
from jax import lax
from jax.sharding import PartitionSpec as P

INST = 8
HB_INST = 7
NB = 6
AGG = 8
BLK = 128
RAD = 3
ITERS = 6


exact_precision = lax.Precision.HIGHEST


def shifted(value, axis, steps):
    count = lax.axis_size(axis)
    pairs = [(source, (source + steps) % count) for source in range(count)]
    return lax.ppermute(value, axis, pairs)


def spectral_matrix():
    row_ids = jnp.arange(INST)[:, None]
    col_ids = jnp.arange(INST)[None, :]
    distance = row_ids - col_ids
    usable = (row_ids < HB_INST) & (col_ids < HB_INST) & (distance != 0)
    parity = 1.0 - 2.0 * jnp.mod(distance, 2).astype(jnp.float32)
    denominator = jnp.sin(jnp.pi * jnp.where(usable, distance, 1).astype(jnp.float32) / HB_INST)
    return jnp.where(usable, 0.5 * parity / denominator, 0.0)


def body(
    fine_residual,
    fine_map,
    routes,
    receive_lists,
    neighbours,
    face_weights,
    spectral_coef,
    diag_extra,
):
    n_cell = lax.axis_size("cell")
    cell_index = lax.axis_index("cell")
    inst_index = lax.axis_index("inst")
    inst_dev, var_count, fine_dev = fine_residual.shape
    blocks = routes.shape[1]
    handed = blocks // 16
    coarse_block = BLK // AGG
    coarse_dev = blocks * coarse_block
    peer_slots = 2 * RAD
    halo_width = receive_lists.shape[1] // peer_slots
    offsets = [slot - RAD if slot < RAD else slot - RAD + 1 for slot in range(peer_slots)]
    relative = jnp.mod(routes[0] - cell_index, n_cell)
    category = jnp.where(relative == 1, 0, jnp.where(relative == 0, 1, 2)).astype(jnp.int32)
    block_ids = jnp.arange(blocks, dtype=jnp.int32)
    lower_class = jnp.sum((category[None, :] < category[:, None]).astype(jnp.int32), axis=1)
    same_before = (category[None, :] == category[:, None]) & (
        block_ids[None, :] < block_ids[:, None]
    )
    position = lower_class + jnp.sum(same_before.astype(jnp.int32), axis=1)
    permuter = (position[:, None] == block_ids[None, :]).astype(jnp.float32)
    cell_map = fine_map.reshape(blocks, BLK)
    one_hot = (
        cell_map[:, :, None] == jnp.arange(coarse_block, dtype=jnp.int32)[None, None, :]
    ).astype(jnp.float32)
    fine_blocks = fine_residual.reshape(inst_dev, var_count, blocks, BLK)
    restricted = jnp.einsum("ivbf,bfc->ivbc", fine_blocks, one_hot, precision=exact_precision)
    ordered = jnp.einsum("ivbc,bq->ivqc", restricted, permuter, precision=exact_precision)
    from_below = shifted(ordered[:, :, :handed], "cell", 1)
    from_above = shifted(ordered[:, :, blocks - handed :], "cell", -1)
    arrived = jnp.concatenate(
        [from_below, ordered[:, :, handed : blocks - handed], from_above], axis=2
    )
    arrived = arrived.reshape(inst_dev, var_count, coarse_dev)
    inst_ids = inst_index * inst_dev + jnp.arange(inst_dev)
    coarse_residual = jnp.where((inst_ids < HB_INST)[:, None, None], arrived, jnp.float32(0.0))
    own_lists = receive_lists[0].reshape(peer_slots, halo_width)
    send_lists = []
    for slot in range(peer_slots):
        send_lists.append(shifted(own_lists[slot], "cell", offsets[slot]))
    all_sends = jnp.concatenate(send_lists, axis=0)
    diagonal = jnp.sum(face_weights, axis=0)[None, :] + 3.0 * spectral_coef[None, :] + diag_extra
    spec_rows = spectral_matrix()[inst_ids]
    correction = coarse_residual / diagonal[None]
    for sweep in range(ITERS):
        outgoing = jnp.take(correction, all_sends, axis=2)
        pieces = []
        for halo_slot in range(peer_slots):
            values = outgoing[:, :, halo_slot * halo_width : (halo_slot + 1) * halo_width]
            pieces.append(shifted(values, "cell", -offsets[halo_slot]))
        extended = jnp.concatenate([correction, jnp.concatenate(pieces, axis=2)], axis=2)
        total = jnp.zeros_like(correction)
        for slot_index in range(NB):
            total = total + face_weights[slot_index][None, None, :] * jnp.take(
                extended, neighbours[slot_index], axis=2
            )
        gathered = lax.all_gather(correction, "inst", axis=0, tiled=True)
        summed = jnp.einsum("nm,mvc->nvc", spec_rows, gathered, precision=exact_precision)
        correction = (coarse_residual + total - spectral_coef[None, None, :] * summed) / diagonal[
            None
        ]
    coarse_blocks = correction.reshape(inst_dev, var_count, blocks, coarse_block)
    back_above = shifted(coarse_blocks[:, :, :handed], "cell", -1)
    back_below = shifted(coarse_blocks[:, :, blocks - handed :], "cell", 1)
    returned = jnp.concatenate(
        [back_above, coarse_blocks[:, :, handed : blocks - handed], back_below], axis=2
    )
    returned_blocks = jnp.einsum("ivqc,bq->ivbc", returned, permuter, precision=exact_precision)
    fine_correction = jnp.einsum(
        "ivbc,bfc->ivbf", returned_blocks, one_hot, precision=exact_precision
    )
    return (fine_correction.reshape(inst_dev, var_count, fine_dev), correction)


def solution(mesh):
    in_specs = (
        P("inst", None, "cell"),
        P("cell"),
        P("cell", None),
        P("cell", None),
        P(None, "cell"),
        P(None, "cell"),
        P("cell"),
        P(None, "cell"),
    )
    out_specs = (P("inst", None, "cell"), P("inst", None, "cell"))
    return jax.shard_map(body, mesh=mesh, in_specs=in_specs, out_specs=out_specs, check_vma=False)
```

profile of v0, /device:TPU:0, one launch (start us, length us, event | category | flops | bytes accessed | tf_op | source)
XLA Modules:
  0.0 390.7 jit_solution(1031421473719623911)
XLA Ops:
  5.7 3.0 collective-permute-start
  8.7 3.1 collective-permute-start.1
  18.3 3.7 collective-permute-start.7
  26.2 3.5 collective-permute-start.10
  33.2 1.9 collective-permute-start.8
  36.5 5.8 %all_gather.18 = f32[8,6,1024]{2,1,0:T(8,128)S(1)} all-gather(f32[2,6,1024]{2,1,0:T(8,128)S(1)} %copy.217), channel_id=1, replica_groups=mesh['cell'=8,'inst'=4] {'inst'}, dimensions={0}, use_global_device_ids=true | all-gather | bytes 245760 | tf_op jit(solution)/shard_map/all_gather | solution.py:99
  43.6 3.6 gather_fusion.2
  47.6 3.6 gather_fusion.3
  51.7 3.6 gather_fusion.4
  55.7 3.6 gather_fusion.5
  59.7 3.6 gather_fusion.6
  63.8 3.6 gather_fusion.7
  71.7 3.0 collective-permute-start.16
  74.7 2.6 collective-permute-start.17
  78.7 6.4 %all_gather.19 = f32[8,6,1024]{2,1,0:T(8,128)} all-gather(f32[2,6,1024]{2,1,0:T(8,128)S(1)} %copy.233), channel_id=1, replica_groups=mesh['cell'=8,'inst'=4] {'inst'}, dimensions={0}, use_global_device_ids=true | all-gather | bytes 245760 | tf_op jit(solution)/shard_map/all_gather | solution.py:99
  86.3 7.6 %gather_fusion.9 = f32[1024,2,6]{2,1,0:T(2,128)} fusion(f32[2,6,1216]{1,0,2:T(2,128)S(1)} %copy.221, s32[1024]{0:T(1024)S(1)} %fusion.89), kind=kCustom, calls=%fused_computation.12.clone | custom fusion | bytes 102400 | tf_op jit(solution)/shard_map/jit(_take)/gather | solution.py:96
  93.9 7.5 %gather_fusion.10 = f32[1024,2,6]{2,1,0:T(2,128)} fusion(f32[2,6,1216]{1,0,2:T(2,128)S(1)} %copy.221, s32[1024]{0:T(1024)S(1)} %fusion.84), kind=kCustom, calls=%fused_computation.13.clone | custom fusion | bytes 102400 | tf_op jit(solution)/shard_map/jit(_take)/gather | solution.py:96
  101.4 7.5 %gather_fusion.11 = f32[1024,2,6]{2,1,0:T(2,128)} fusion(f32[2,6,1216]{1,0,2:T(2,128)S(1)} %copy.221, s32[1024]{0:T(1024)S(1)} %fusion.85), kind=kCustom, calls=%fused_computation.14.clone | custom fusion | bytes 102400 | tf_op jit(solution)/shard_map/jit(_take)/gather | solution.py:96
  109.0 7.5 %gather_fusion.12 = f32[1024,2,6]{2,1,0:T(2,128)} fusion(f32[2,6,1216]{1,0,2:T(2,128)S(1)} %copy.221, s32[1024]{0:T(1024)S(1)} %fusion.86), kind=kCustom, calls=%fused_computation.15.clone | custom fusion | bytes 102400 | tf_op jit(solution)/shard_map/jit(_take)/gather | solution.py:96
  116.5 3.5 gather_fusion.13
  120.0 3.5 gather_fusion.14
  125.0 1.5 copy.224
  131.8 2.5 collective-permute-start.20
  136.9 3.2 collective-permute-start.23
  141.6 6.2 %all_gather.20 = f32[8,6,1024]{2,1,0:T(8,128)} all-gather(f32[2,6,1024]{2,1,0:T(8,128)S(1)} %copy.249), channel_id=1, replica_groups=mesh['cell'=8,'inst'=4] {'inst'}, dimensions={0}, use_global_device_ids=true | all-gather | bytes 245760 | tf_op jit(solution)/shard_map/all_gather | solution.py:99
  149.1 7.6 %gather_fusion.16 = f32[1024,2,6]{2,1,0:T(2,128)} fusion(f32[2,6,1216]{1,0,2:T(2,128)S(1)} %copy.237, s32[1024]{0:T(1024)S(1)} %fusion.89), kind=kCustom, calls=%fused_computation.18.clone | custom fusion | bytes 102400 | tf_op jit(solution)/shard_map/jit(_take)/gather | solution.py:96
  156.6 7.5 %gather_fusion.17 = f32[1024,2,6]{2,1,0:T(2,128)} fusion(f32[2,6,1216]{1,0,2:T(2,128)S(1)} %copy.237, s32[1024]{0:T(1024)S(1)} %fusion.84), kind=kCustom, calls=%fused_computation.19.clone | custom fusion | bytes 102400 | tf_op jit(solution)/shard_map/jit(_take)/gather | solution.py:96
  164.2 7.5 %gather_fusion.18 = f32[1024,2,6]{2,1,0:T(2,128)} fusion(f32[2,6,1216]{1,0,2:T(2,128)S(1)} %copy.237, s32[1024]{0:T(1024)S(1)} %fusion.85), kind=kCustom, calls=%fused_computation.20.clone | custom fusion | bytes 102400 | tf_op jit(solution)/shard_map/jit(_take)/gather | solution.py:96
  171.7 7.5 %gather_fusion.19 = f32[1024,2,6]{2,1,0:T(2,128)} fusion(f32[2,6,1216]{1,0,2:T(2,128)S(1)} %copy.237, s32[1024]{0:T(1024)S(1)} %fusion.86), kind=kCustom, calls=%fused_computation.21.clone | custom fusion | bytes 102400 | tf_op jit(solution)/shard_map/jit(_take)/gather | solution.py:96
  179.2 3.5 gather_fusion.20
  182.8 3.5 gather_fusion.21
  187.8 1.5 copy.240
  194.4 2.5 collective-permute-start.26
  199.6 3.2 collective-permute-start.29
  204.3 6.4 %all_gather.21 = f32[8,6,1024]{2,1,0:T(8,128)} all-gather(f32[2,6,1024]{2,1,0:T(8,128)S(1)} %copy.265), channel_id=1, replica_groups=mesh['cell'=8,'inst'=4] {'inst'}, dimensions={0}, use_global_device_ids=true | all-gather | bytes 245760 | tf_op jit(solution)/shard_map/all_gather | solution.py:99
  212.0 7.6 %gather_fusion.23 = f32[1024,2,6]{2,1,0:T(2,128)} fusion(f32[2,6,1216]{1,0,2:T(2,128)S(1)} %copy.253, s32[1024]{0:T(1024)S(1)} %fusion.89), kind=kCustom, calls=%fused_computation.24.clone | custom fusion | bytes 102400 | tf_op jit(solution)/shard_map/jit(_take)/gather | solution.py:96
  219.6 7.5 %gather_fusion.24 = f32[1024,2,6]{2,1,0:T(2,128)} fusion(f32[2,6,1216]{1,0,2:T(2,128)S(1)} %copy.253, s32[1024]{0:T(1024)S(1)} %fusion.84), kind=kCustom, calls=%fused_computation.25.clone | custom fusion | bytes 102400 | tf_op jit(solution)/shard_map/jit(_take)/gather | solution.py:96
  227.1 7.5 %gather_fusion.25 = f32[1024,2,6]{2,1,0:T(2,128)} fusion(f32[2,6,1216]{1,0,2:T(2,128)S(1)} %copy.253, s32[1024]{0:T(1024)S(1)} %fusion.85), kind=kCustom, calls=%fused_computation.26.clone | custom fusion | bytes 102400 | tf_op jit(solution)/shard_map/jit(_take)/gather | solution.py:96
  234.6 7.5 %gather_fusion.26 = f32[1024,2,6]{2,1,0:T(2,128)} fusion(f32[2,6,1216]{1,0,2:T(2,128)S(1)} %copy.253, s32[1024]{0:T(1024)S(1)} %fusion.86), kind=kCustom, calls=%fused_computation.27.clone | custom fusion | bytes 102400 | tf_op jit(solution)/shard_map/jit(_take)/gather | solution.py:96
  242.1 3.5 gather_fusion.27
  245.7 3.5 gather_fusion.28
  250.7 1.5 copy.256
  257.4 2.5 collective-permute-start.32
  262.6 3.2 collective-permute-start.35
  267.2 6.2 %all_gather.22 = f32[8,6,1024]{2,1,0:T(8,128)} all-gather(f32[2,6,1024]{2,1,0:T(8,128)S(1)} %copy.281), channel_id=1, replica_groups=mesh['cell'=8,'inst'=4] {'inst'}, dimensions={0}, use_global_device_ids=true | all-gather | bytes 245760 | tf_op jit(solution)/shard_map/all_gather | solution.py:99
  274.7 7.6 %gather_fusion.30 = f32[1024,2,6]{2,1,0:T(2,128)} fusion(f32[2,6,1216]{1,0,2:T(2,128)S(1)} %copy.269, s32[1024]{0:T(1024)S(1)} %fusion.89), kind=kCustom, calls=%fused_computation.30.clone | custom fusion | bytes 102400 | tf_op jit(solution)/shard_map/jit(_take)/gather | solution.py:96
  282.2 7.5 %gather_fusion.31 = f32[1024,2,6]{2,1,0:T(2,128)} fusion(f32[2,6,1216]{1,0,2:T(2,128)S(1)} %copy.269, s32[1024]{0:T(1024)S(1)} %fusion.84), kind=kCustom, calls=%fused_computation.31.clone | custom fusion | bytes 102400 | tf_op jit(solution)/shard_map/jit(_take)/gather | solution.py:96
  289.8 7.5 %gather_fusion.32 = f32[1024,2,6]{2,1,0:T(2,128)} fusion(f32[2,6,1216]{1,0,2:T(2,128)S(1)} %copy.269, s32[1024]{0:T(1024)S(1)} %fusion.85), kind=kCustom, calls=%fused_computation.32.clone | custom fusion | bytes 102400 | tf_op jit(solution)/shard_map/jit(_take)/gather | solution.py:96
  297.3 7.5 %gather_fusion.33 = f32[1024,2,6]{2,1,0:T(2,128)} fusion(f32[2,6,1216]{1,0,2:T(2,128)S(1)} %copy.269, s32[1024]{0:T(1024)S(1)} %fusion.86), kind=kCustom, calls=%fused_computation.33.clone | custom fusion | bytes 102400 | tf_op jit(solution)/shard_map/jit(_take)/gather | solution.py:96
  304.8 3.5 gather_fusion.34
  308.4 3.5 gather_fusion.35
  313.4 1.5 copy.272
  320.1 2.5 collective-permute-start.38
  325.3 3.3 collective-permute-start.41
  329.9 6.5 %all_gather.23 = f32[8,6,1024]{2,1,0:T(8,128)} all-gather(f32[2,6,1024]{2,1,0:T(8,128)S(1)} %copy.297), channel_id=1, replica_groups=mesh['cell'=8,'inst'=4] {'inst'}, dimensions={0}, use_global_device_ids=true | all-gather | bytes 245760 | tf_op jit(solution)/shard_map/all_gather | solution.py:99
  337.7 3.6 gather_fusion.37
  341.2 3.6 gather_fusion.38
  344.8 7.6 %gather_fusion.39 = f32[1024,2,6]{2,1,0:T(2,128)} fusion(f32[2,6,1216]{1,0,2:T(2,128)S(1)} %copy.285, s32[1024]{0:T(1024)S(1)} %fusion.85), kind=kCustom, calls=%fused_computation.38.clone | custom fusion | bytes 102400 | tf_op jit(solution)/shard_map/jit(_take)/gather | solution.py:96
  352.4 7.5 %gather_fusion.40 = f32[1024,2,6]{2,1,0:T(2,128)} fusion(f32[2,6,1216]{1,0,2:T(2,128)S(1)} %copy.285, s32[1024]{0:T(1024)S(1)} %fusion.86), kind=kCustom, calls=%fused_computation.39.clone | custom fusion | bytes 102400 | tf_op jit(solution)/shard_map/jit(_take)/gather | solution.py:96
  359.9 7.5 %gather_fusion.41 = f32[1024,2,6]{2,1,0:T(2,128)} fusion(f32[2,6,1216]{1,0,2:T(2,128)S(1)} %copy.285, s32[1024]{0:T(1024)S(1)} %fusion.87), kind=kCustom, calls=%fused_computation.40.clone | custom fusion | bytes 102400 | tf_op jit(solution)/shard_map/jit(_take)/gather | solution.py:96
  367.4 7.5 %gather_fusion.42 = f32[1024,2,6]{2,1,0:T(2,128)} fusion(f32[2,6,1216]{1,0,2:T(2,128)S(1)} %copy.285, s32[1024]{0:T(1024)S(1)} %fusion.88), kind=kCustom, calls=%fused_computation.41.clone | custom fusion | bytes 102400 | tf_op jit(solution)/shard_map/jit(_take)/gather | solution.py:96
  379.5 2.4 collective-permute-start.44
  382.7 1.6 collective-permute-done.44
  384.4 4.0 %collective-permute-done.45 = f32[2,6,4,16]{3,2,0,1:T(4,128)S(1)} collective-permute-done((f32[2,6,4,16]{3,2,0,1:T(4,128)S(1)}, f32[2,6,4,16]{3,2,0,1:T(4,128)S(1)}, u32[]{:S(2)}, u32[]{:S(2)}) %collective-permute-start.45) | collective-permute-done | bytes 3104 | tf_op jit(solution)/shard_map/ppermute | solution.py:21
  (333 shorter events, 85.5 us)
Async XLA Ops:
  2.0 13.6 %copy-start.17 = (s32[6,1024]{1,0:T(8,128)S(1)}, s32[6,1024]{1,0:T(8,128)}, u32[]{:S(2)}) copy-start(s32[6,1024]{1,0:T(8,128)} %param.16) | copy-start | bytes 73732
  3.3 12.5 %copy-start.14 = (f32[6,1024]{1,0:T(8,128)S(1)}, f32[6,1024]{1,0:T(8,128)}, u32[]{:S(2)}) copy-start(f32[6,1024]{1,0:T(8,128)} %param.17) | copy-start | bytes 73732
  3.3 12.7 %copy-start.19 = (f32[1024]{0:T(1024)S(1)}, f32[1024]{0:T(1024)}, u32[]{:S(2)}) copy-start(f32[1024]{0:T(1024)} %param.18) | copy-start | bytes 12292
  3.4 12.8 %copy-start.16 = (f32[6,1024]{1,0:T(8,128)S(1)}, f32[6,1024]{1,0:T(8,128)}, u32[]{:S(2)}) copy-start(f32[6,1024]{1,0:T(8,128)} %param.19) | copy-start | bytes 73732
  3.6 12.4 %copy-start.30 = (s32[64]{0:T(128)}, s32[64]{0:T(128)S(1)}, u32[]{:S(2)}) copy-start(s32[64]{0:T(128)S(1)} %add.191) | copy-start | bytes 772
  5.7 18.2 %collective-permute-start = (f32[2,6,4,16]{2,3,1,0:T(8,128)S(1)}, f32[2,6,4,16]{2,3,1,0:T(8,128)S(1)}, u32[]{:S(2)}, u32[]{:S(2)}) collective-permute-start(f32[2,6,4,16]{2,3,1,0:T(8,128)S(1)} %get-tuple-element.8), channel_id=1, source_target_pairs={{0,4},{4,8},{8,12},{12,16},{16,20},{20,24},{24,28},{28,0},{1,5},{5... | collective-permute-start | bytes 9224 | tf_op jit(solution)/shard_map/ppermute | solution.py:21
  8.7 15.1 %collective-permute-start.1 = (f32[2,6,4,16]{2,3,1,0:T(8,128)S(1)}, f32[2,6,4,16]{2,3,1,0:T(8,128)S(1)}, u32[]{:S(2)}, u32[]{:S(2)}) collective-permute-start(f32[2,6,4,16]{2,3,1,0:T(8,128)S(1)} %get-tuple-element.9), channel_id=1, source_target_pairs={{0,28},{4,0},{8,4},{12,8},{16,12},{20,16},{24,20},{28,24},{1,29},{... | collective-permute-start | bytes 9224 | tf_op jit(solution)/shard_map/ppermute | solution.py:21
  11.9 4.5 %collective-permute-start.2 = (s32[32]{0:T(128)S(1)}, s32[32]{0:T(128)S(1)}, u32[]{:S(2)}, u32[]{:S(2)}) collective-permute-start(s32[32]{0:T(128)S(1)} %get-tuple-element.62), channel_id=1, source_target_pairs={{0,20},{4,24},{8,28},{12,0},{16,4},{20,8},{24,12},{28,16},{1,21},{... | collective-permute-start | bytes 392 | tf_op jit(solution)/shard_map/ppermute | solution.py:21
  12.8 4.1 %collective-permute-start.3 = (s32[32]{0:T(128)S(1)}, s32[32]{0:T(128)S(1)}, u32[]{:S(2)}, u32[]{:S(2)}) collective-permute-start(s32[32]{0:T(128)S(1)} %get-tuple-element.61), channel_id=1, source_target_pairs={{0,24},{4,28},{8,0},{12,4},{16,8},{20,12},{24,16},{28,20},{1,25},{... | collective-permute-start | bytes 392 | tf_op jit(solution)/shard_map/ppermute | solution.py:21
  14.2 4.2 %collective-permute-start.4 = (s32[32]{0:T(128)S(1)}, s32[32]{0:T(128)S(1)}, u32[]{:S(2)}, u32[]{:S(2)}) collective-permute-start(s32[32]{0:T(128)S(1)} %get-tuple-element.60), channel_id=1, source_target_pairs={{0,28},{4,0},{8,4},{12,8},{16,12},{20,16},{24,20},{28,24},{1,29},{... | collective-permute-start | bytes 392 | tf_op jit(solution)/shard_map/ppermute | solution.py:21
  15.7 302.1 %copy-start.32 = (pred[1024]{0:T(1024)(128)(4,1)}, pred[1024]{0:T(1024)(128)(4,1)S(1)}, u32[]{:S(2)}) copy-start(pred[1024]{0:T(1024)(128)(4,1)S(1)} %get-tuple-element.64) | copy-start | bytes 3076
  15.7 302.1 %copy-start.34 = (pred[1024]{0:T(1024)(128)(4,1)}, pred[1024]{0:T(1024)(128)(4,1)S(1)}, u32[]{:S(2)}) copy-start(pred[1024]{0:T(1024)(128)(4,1)S(1)} %get-tuple-element.65) | copy-start | bytes 3076
  15.7 52.1 %copy-start.38 = (pred[1024]{0:T(1024)(128)(4,1)}, pred[1024]{0:T(1024)(128)(4,1)S(1)}, u32[]{:S(2)}) copy-start(pred[1024]{0:T(1024)(128)(4,1)S(1)} %get-tuple-element.67) | copy-start | bytes 3076
  15.7 302.1 %copy-start.36 = (pred[1024]{0:T(1024)(128)(4,1)}, pred[1024]{0:T(1024)(128)(4,1)S(1)}, u32[]{:S(2)}) copy-start(pred[1024]{0:T(1024)(128)(4,1)S(1)} %get-tuple-element.66) | copy-start | bytes 3076
  15.8 52.0 %copy-start.41 = (pred[1024]{0:T(1024)(128)(4,1)}, pred[1024]{0:T(1024)(128)(4,1)S(1)}, u32[]{:S(2)}) copy-start(pred[1024]{0:T(1024)(128)(4,1)S(1)} %get-tuple-element.68) | copy-start | bytes 3076
  15.8 52.0 %copy-start.44 = (pred[1024]{0:T(1024)(128)(4,1)}, pred[1024]{0:T(1024)(128)(4,1)S(1)}, u32[]{:S(2)}) copy-start(pred[1024]{0:T(1024)(128)(4,1)S(1)} %get-tuple-element.69) | copy-start | bytes 3076
  15.8 52.0 %copy-start.56 = (pred[2]{0:T(512)(128)(4,1)}, pred[2]{0:T(512)(128)(4,1)S(1)}, u32[]{:S(2)}) copy-start(pred[2]{0:T(512)(128)(4,1)S(1)} %add_compare_fusion) | copy-start | bytes 10
  15.9 301.9 %copy-start.20 = (f32[1,1024]{1,0:T(1,128)}, f32[1,1024]{1,0:T(1,128)S(1)}, u32[]{:S(2)}) copy-start(f32[1,1024]{1,0:T(1,128)S(1)} %get-tuple-element.11) | copy-start | bytes 12292
  15.9 301.9 %copy-start.22 = (f32[1,1024]{1,0:T(1,128)}, f32[1,1024]{1,0:T(1,128)S(1)}, u32[]{:S(2)}) copy-start(f32[1,1024]{1,0:T(1,128)S(1)} %get-tuple-element.12) | copy-start | bytes 12292
  15.9 301.9 %copy-start.24 = (f32[1,1024]{1,0:T(1,128)}, f32[1,1024]{1,0:T(1,128)S(1)}, u32[]{:S(2)}) copy-start(f32[1,1024]{1,0:T(1,128)S(1)} %get-tuple-element.13) | copy-start | bytes 12292
  15.9 301.9 %copy-start.26 = (f32[1,1024]{1,0:T(1,128)}, f32[1,1024]{1,0:T(1,128)S(1)}, u32[]{:S(2)}) copy-start(f32[1,1024]{1,0:T(1,128)S(1)} %get-tuple-element.14) | copy-start | bytes 12292
  15.9 301.9 %copy-start.28 = (f32[1,1024]{1,0:T(1,128)}, f32[1,1024]{1,0:T(1,128)S(1)}, u32[]{:S(2)}) copy-start(f32[1,1024]{1,0:T(1,128)S(1)} %get-tuple-element.15) | copy-start | bytes 12292
  16.4 6.3 %collective-permute-start.5 = (s32[32]{0:T(128)S(1)}, s32[32]{0:T(128)S(1)}, u32[]{:S(2)}, u32[]{:S(2)}) collective-permute-start(s32[32]{0:T(128)S(1)} %get-tuple-element.59), channel_id=1, source_target_pairs={{0,4},{4,8},{8,12},{12,16},{16,20},{20,24},{24,28},{28,0},{1,5},{5... | collective-permute-start | bytes 392 | tf_op jit(solution)/shard_map/ppermute | solution.py:21
  16.9 5.7 %collective-permute-start.6 = (s32[32]{0:T(128)S(1)}, s32[32]{0:T(128)S(1)}, u32[]{:S(2)}, u32[]{:S(2)}) collective-permute-start(s32[32]{0:T(128)S(1)} %get-tuple-element.63), channel_id=1, source_target_pairs={{0,8},{4,12},{8,16},{12,20},{16,24},{20,28},{24,0},{28,4},{1,9},{5... | collective-permute-start | bytes 392 | tf_op jit(solution)/shard_map/ppermute | solution.py:21
  18.3 5.4 %collective-permute-start.7 = (s32[32]{0:T(128)S(1)}, s32[32]{0:T(128)S(1)}, u32[]{:S(2)}, u32[]{:S(2)}) collective-permute-start(s32[32]{0:T(128)S(1)} %get-tuple-element.58), channel_id=1, source_target_pairs={{0,12},{4,16},{8,20},{12,24},{16,28},{20,0},{24,4},{28,8},{1,13},{... | collective-permute-start | bytes 392 | tf_op jit(solution)/shard_map/ppermute | solution.py:21
  26.2 9.0 %collective-permute-start.10 = (f32[2,6,32]{2,0,1:T(2,128)S(1)}, f32[2,6,32]{2,0,1:T(2,128)S(1)}, u32[]{:S(2)}, u32[]{:S(2)}) collective-permute-start(f32[2,6,32]{2,0,1:T(2,128)S(1)} %get-tuple-element.55), channel_id=1, source_target_pairs={{0,4},{4,8},{8,12},{12,16},{16,20},{20,24},{24,28},{28,0},{1,5},{5... | collective-permute-start | bytes 4616 | tf_op jit(solution)/shard_map/ppermute | solution.py:21
  30.2 37.6 %copy-start.50 = (f32[2,8]{1,0:T(2,128)}, f32[2,8]{1,0:T(2,128)S(1)}, u32[]{:S(2)}) copy-start(f32[2,8]{1,0:T(2,128)S(1)} %gather_fusion) | copy-start | bytes 196
  30.3 12.0 %collective-permute-start.11 = (f32[2,6,32]{2,0,1:T(2,128)S(1)}, f32[2,6,32]{2,0,1:T(2,128)S(1)}, u32[]{:S(2)}, u32[]{:S(2)}) collective-permute-start(f32[2,6,32]{2,0,1:T(2,128)S(1)} %get-tuple-element.54), channel_id=1, source_target_pairs={{0,28},{4,0},{8,4},{12,8},{16,12},{20,16},{24,20},{28,24},{1,29},{... | collective-permute-start | bytes 4616 | tf_op jit(solution)/shard_map/ppermute | solution.py:21
  31.6 10.7 %collective-permute-start.12 = (f32[2,6,32]{2,0,1:T(2,128)S(1)}, f32[2,6,32]{2,0,1:T(2,128)S(1)}, u32[]{:S(2)}, u32[]{:S(2)}) collective-permute-start(f32[2,6,32]{2,0,1:T(2,128)S(1)} %get-tuple-element.53), channel_id=1, source_target_pairs={{0,24},{4,28},{8,0},{12,4},{16,8},{20,12},{24,16},{28,20},{1,25},{... | collective-permute-start | bytes 4616 | tf_op jit(solution)/shard_map/ppermute | solution.py:21
  32.2 10.1 %collective-permute-start.13 = (f32[2,6,32]{2,0,1:T(2,128)S(1)}, f32[2,6,32]{2,0,1:T(2,128)S(1)}, u32[]{:S(2)}, u32[]{:S(2)}) collective-permute-start(f32[2,6,32]{2,0,1:T(2,128)S(1)} %get-tuple-element.52), channel_id=1, source_target_pairs={{0,20},{4,24},{8,28},{12,0},{16,4},{20,8},{24,12},{28,16},{1,21},{... | collective-permute-start | bytes 4616 | tf_op jit(solution)/shard_map/ppermute | solution.py:21
  33.2 9.1 %collective-permute-start.8 = (f32[2,6,32]{2,0,1:T(2,128)S(1)}, f32[2,6,32]{2,0,1:T(2,128)S(1)}, u32[]{:S(2)}, u32[]{:S(2)}) collective-permute-start(f32[2,6,32]{2,0,1:T(2,128)S(1)} %get-tuple-element.57), channel_id=1, source_target_pairs={{0,12},{4,16},{8,20},{12,24},{16,28},{20,0},{24,4},{28,8},{1,13},{... | collective-permute-start | bytes 4616 | tf_op jit(solution)/shard_map/ppermute | solution.py:21
  35.1 7.2 %collective-permute-start.9 = (f32[2,6,32]{2,0,1:T(2,128)S(1)}, f32[2,6,32]{2,0,1:T(2,128)S(1)}, u32[]{:S(2)}, u32[]{:S(2)}) collective-permute-start(f32[2,6,32]{2,0,1:T(2,128)S(1)} %get-tuple-element.56), channel_id=1, source_target_pairs={{0,8},{4,12},{8,16},{12,20},{16,24},{20,28},{24,0},{28,4},{1,9},{5... | collective-permute-start | bytes 4616 | tf_op jit(solution)/shard_map/ppermute | solution.py:21
  70.1 8.1 %collective-permute-start.14 = (f32[2,6,32]{2,0,1:T(2,128)S(1)}, f32[2,6,32]{2,0,1:T(2,128)S(1)}, u32[]{:S(2)}, u32[]{:S(2)}) collective-permute-start(f32[2,6,32]{2,0,1:T(2,128)S(1)} %get-tuple-element.51), channel_id=1, source_target_pairs={{0,12},{4,16},{8,20},{12,24},{16,28},{20,0},{24,4},{28,8},{1,13},{... | collective-permute-start | bytes 4616 | tf_op jit(solution)/shard_map/ppermute | solution.py:21
  71.3 13.8 %collective-permute-start.15 = (f32[2,6,32]{2,0,1:T(2,128)S(1)}, f32[2,6,32]{2,0,1:T(2,128)S(1)}, u32[]{:S(2)}, u32[]{:S(2)}) collective-permute-start(f32[2,6,32]{2,0,1:T(2,128)S(1)} %get-tuple-element.50), channel_id=1, source_target_pairs={{0,8},{4,12},{8,16},{12,20},{16,24},{20,28},{24,0},{28,4},{1,9},{5... | collective-permute-start | bytes 4616 | tf_op jit(solution)/shard_map/ppermute | solution.py:21
  71.7 13.4 %collective-permute-start.16 = (f32[2,6,32]{2,0,1:T(2,128)S(1)}, f32[2,6,32]{2,0,1:T(2,128)S(1)}, u32[]{:S(2)}, u32[]{:S(2)}) collective-permute-start(f32[2,6,32]{2,0,1:T(2,128)S(1)} %get-tuple-element.49), channel_id=1, source_target_pairs={{0,4},{4,8},{8,12},{12,16},{16,20},{20,24},{24,28},{28,0},{1,5},{5... | collective-permute-start | bytes 4616 | tf_op jit(solution)/shard_map/ppermute | solution.py:21
  74.7 10.4 %collective-permute-start.17 = (f32[2,6,32]{2,0,1:T(2,128)S(1)}, f32[2,6,32]{2,0,1:T(2,128)S(1)}, u32[]{:S(2)}, u32[]{:S(2)}) collective-permute-start(f32[2,6,32]{2,0,1:T(2,128)S(1)} %get-tuple-element.48), channel_id=1, source_target_pairs={{0,28},{4,0},{8,4},{12,8},{16,12},{20,16},{24,20},{28,24},{1,29},{... | collective-permute-start | bytes 4616 | tf_op jit(solution)/shard_map/ppermute | solution.py:21
  77.2 7.8 %collective-permute-start.18 = (f32[2,6,32]{2,0,1:T(2,128)S(1)}, f32[2,6,32]{2,0,1:T(2,128)S(1)}, u32[]{:S(2)}, u32[]{:S(2)}) collective-permute-start(f32[2,6,32]{2,0,1:T(2,128)S(1)} %get-tuple-element.47), channel_id=1, source_target_pairs={{0,24},{4,28},{8,0},{12,4},{16,8},{20,12},{24,16},{28,20},{1,25},{... | collective-permute-start | bytes 4616 | tf_op jit(solution)/shard_map/ppermute | solution.py:21
  78.2 6.9 %collective-permute-start.19 = (f32[2,6,32]{2,0,1:T(2,128)S(1)}, f32[2,6,32]{2,0,1:T(2,128)S(1)}, u32[]{:S(2)}, u32[]{:S(2)}) collective-permute-start(f32[2,6,32]{2,0,1:T(2,128)S(1)} %get-tuple-element.46), channel_id=1, source_target_pairs={{0,20},{4,24},{8,28},{12,0},{16,4},{20,8},{24,12},{28,16},{1,21},{... | collective-permute-start | bytes 4616 | tf_op jit(solution)/shard_map/ppermute | solution.py:21
  131.8 9.3 %collective-permute-start.20 = (f32[2,6,32]{2,0,1:T(2,128)S(1)}, f32[2,6,32]{2,0,1:T(2,128)S(1)}, u32[]{:S(2)}, u32[]{:S(2)}) collective-permute-start(f32[2,6,32]{2,0,1:T(2,128)S(1)} %get-tuple-element.45), channel_id=1, source_target_pairs={{0,12},{4,16},{8,20},{12,24},{16,28},{20,0},{24,4},{28,8},{1,13},{... | collective-permute-start | bytes 4616 | tf_op jit(solution)/shard_map/ppermute | solution.py:21
  134.3 13.5 %collective-permute-start.21 = (f32[2,6,32]{2,0,1:T(2,128)S(1)}, f32[2,6,32]{2,0,1:T(2,128)S(1)}, u32[]{:S(2)}, u32[]{:S(2)}) collective-permute-start(f32[2,6,32]{2,0,1:T(2,128)S(1)} %get-tuple-element.44), channel_id=1, source_target_pairs={{0,8},{4,12},{8,16},{12,20},{16,24},{20,28},{24,0},{28,4},{1,9},{5... | collective-permute-start | bytes 4616 | tf_op jit(solution)/shard_map/ppermute | solution.py:21
  135.4 12.4 %collective-permute-start.22 = (f32[2,6,32]{2,0,1:T(2,128)S(1)}, f32[2,6,32]{2,0,1:T(2,128)S(1)}, u32[]{:S(2)}, u32[]{:S(2)}) collective-permute-start(f32[2,6,32]{2,0,1:T(2,128)S(1)} %get-tuple-element.43), channel_id=1, source_target_pairs={{0,4},{4,8},{8,12},{12,16},{16,20},{20,24},{24,28},{28,0},{1,5},{5... | collective-permute-start | bytes 4616 | tf_op jit(solution)/shard_map/ppermute | solution.py:21
  136.9 10.8 %collective-permute-start.23 = (f32[2,6,32]{2,0,1:T(2,128)S(1)}, f32[2,6,32]{2,0,1:T(2,128)S(1)}, u32[]{:S(2)}, u32[]{:S(2)}) collective-permute-start(f32[2,6,32]{2,0,1:T(2,128)S(1)} %get-tuple-element.42), channel_id=1, source_target_pairs={{0,28},{4,0},{8,4},{12,8},{16,12},{20,16},{24,20},{28,24},{1,29},{... | collective-permute-start | bytes 4616 | tf_op jit(solution)/shard_map/ppermute | solution.py:21
  140.2 7.6 %collective-permute-start.24 = (f32[2,6,32]{2,0,1:T(2,128)S(1)}, f32[2,6,32]{2,0,1:T(2,128)S(1)}, u32[]{:S(2)}, u32[]{:S(2)}) collective-permute-start(f32[2,6,32]{2,0,1:T(2,128)S(1)} %get-tuple-element.41), channel_id=1, source_target_pairs={{0,24},{4,28},{8,0},{12,4},{16,8},{20,12},{24,16},{28,20},{1,25},{... | collective-permute-start | bytes 4616 | tf_op jit(solution)/shard_map/ppermute | solution.py:21
  141.1 6.7 %collective-permute-start.25 = (f32[2,6,32]{2,0,1:T(2,128)S(1)}, f32[2,6,32]{2,0,1:T(2,128)S(1)}, u32[]{:S(2)}, u32[]{:S(2)}) collective-permute-start(f32[2,6,32]{2,0,1:T(2,128)S(1)} %get-tuple-element.40), channel_id=1, source_target_pairs={{0,20},{4,24},{8,28},{12,0},{16,4},{20,8},{24,12},{28,16},{1,21},{... | collective-permute-start | bytes 4616 | tf_op jit(solution)/shard_map/ppermute | solution.py:21
  194.4 9.3 %collective-permute-start.26 = (f32[2,6,32]{2,0,1:T(2,128)S(1)}, f32[2,6,32]{2,0,1:T(2,128)S(1)}, u32[]{:S(2)}, u32[]{:S(2)}) collective-permute-start(f32[2,6,32]{2,0,1:T(2,128)S(1)} %get-tuple-element.39), channel_id=1, source_target_pairs={{0,12},{4,16},{8,20},{12,24},{16,28},{20,0},{24,4},{28,8},{1,13},{... | collective-permute-start | bytes 4616 | tf_op jit(solution)/shard_map/ppermute | solution.py:21
  197.0 13.7 %collective-permute-start.27 = (f32[2,6,32]{2,0,1:T(2,128)S(1)}, f32[2,6,32]{2,0,1:T(2,128)S(1)}, u32[]{:S(2)}, u32[]{:S(2)}) collective-permute-start(f32[2,6,32]{2,0,1:T(2,128)S(1)} %get-tuple-element.38), channel_id=1, source_target_pairs={{0,8},{4,12},{8,16},{12,20},{16,24},{20,28},{24,0},{28,4},{1,9},{5... | collective-permute-start | bytes 4616 | tf_op jit(solution)/shard_map/ppermute | solution.py:21
  198.1 12.6 %collective-permute-start.28 = (f32[2,6,32]{2,0,1:T(2,128)S(1)}, f32[2,6,32]{2,0,1:T(2,128)S(1)}, u32[]{:S(2)}, u32[]{:S(2)}) collective-permute-start(f32[2,6,32]{2,0,1:T(2,128)S(1)} %get-tuple-element.37), channel_id=1, source_target_pairs={{0,4},{4,8},{8,12},{12,16},{16,20},{20,24},{24,28},{28,0},{1,5},{5... | collective-permute-start | bytes 4616 | tf_op jit(solution)/shard_map/ppermute | solution.py:21
  199.6 11.1 %collective-permute-start.29 = (f32[2,6,32]{2,0,1:T(2,128)S(1)}, f32[2,6,32]{2,0,1:T(2,128)S(1)}, u32[]{:S(2)}, u32[]{:S(2)}) collective-permute-start(f32[2,6,32]{2,0,1:T(2,128)S(1)} %get-tuple-element.36), channel_id=1, source_target_pairs={{0,28},{4,0},{8,4},{12,8},{16,12},{20,16},{24,20},{28,24},{1,29},{... | collective-permute-start | bytes 4616 | tf_op jit(solution)/shard_map/ppermute | solution.py:21
  202.9 7.8 %collective-permute-start.30 = (f32[2,6,32]{2,0,1:T(2,128)S(1)}, f32[2,6,32]{2,0,1:T(2,128)S(1)}, u32[]{:S(2)}, u32[]{:S(2)}) collective-permute-start(f32[2,6,32]{2,0,1:T(2,128)S(1)} %get-tuple-element.35), channel_id=1, source_target_pairs={{0,24},{4,28},{8,0},{12,4},{16,8},{20,12},{24,16},{28,20},{1,25},{... | collective-permute-start | bytes 4616 | tf_op jit(solution)/shard_map/ppermute | solution.py:21
  203.8 6.9 %collective-permute-start.31 = (f32[2,6,32]{2,0,1:T(2,128)S(1)}, f32[2,6,32]{2,0,1:T(2,128)S(1)}, u32[]{:S(2)}, u32[]{:S(2)}) collective-permute-start(f32[2,6,32]{2,0,1:T(2,128)S(1)} %get-tuple-element.34), channel_id=1, source_target_pairs={{0,20},{4,24},{8,28},{12,0},{16,4},{20,8},{24,12},{28,16},{1,21},{... | collective-permute-start | bytes 4616 | tf_op jit(solution)/shard_map/ppermute | solution.py:21
  257.4 9.3 %collective-permute-start.32 = (f32[2,6,32]{2,0,1:T(2,128)S(1)}, f32[2,6,32]{2,0,1:T(2,128)S(1)}, u32[]{:S(2)}, u32[]{:S(2)}) collective-permute-start(f32[2,6,32]{2,0,1:T(2,128)S(1)} %get-tuple-element.33), channel_id=1, source_target_pairs={{0,12},{4,16},{8,20},{12,24},{16,28},{20,0},{24,4},{28,8},{1,13},{... | collective-permute-start | bytes 4616 | tf_op jit(solution)/shard_map/ppermute | solution.py:21
  259.9 13.5 %collective-permute-start.33 = (f32[2,6,32]{2,0,1:T(2,128)S(1)}, f32[2,6,32]{2,0,1:T(2,128)S(1)}, u32[]{:S(2)}, u32[]{:S(2)}) collective-permute-start(f32[2,6,32]{2,0,1:T(2,128)S(1)} %get-tuple-element.32), channel_id=1, source_target_pairs={{0,8},{4,12},{8,16},{12,20},{16,24},{20,28},{24,0},{28,4},{1,9},{5... | collective-permute-start | bytes 4616 | tf_op jit(solution)/shard_map/ppermute | solution.py:21
  261.1 12.3 %collective-permute-start.34 = (f32[2,6,32]{2,0,1:T(2,128)S(1)}, f32[2,6,32]{2,0,1:T(2,128)S(1)}, u32[]{:S(2)}, u32[]{:S(2)}) collective-permute-start(f32[2,6,32]{2,0,1:T(2,128)S(1)} %get-tuple-element.31), channel_id=1, source_target_pairs={{0,4},{4,8},{8,12},{12,16},{16,20},{20,24},{24,28},{28,0},{1,5},{5... | collective-permute-start | bytes 4616 | tf_op jit(solution)/shard_map/ppermute | solution.py:21
  262.6 10.8 %collective-permute-start.35 = (f32[2,6,32]{2,0,1:T(2,128)S(1)}, f32[2,6,32]{2,0,1:T(2,128)S(1)}, u32[]{:S(2)}, u32[]{:S(2)}) collective-permute-start(f32[2,6,32]{2,0,1:T(2,128)S(1)} %get-tuple-element.30), channel_id=1, source_target_pairs={{0,28},{4,0},{8,4},{12,8},{16,12},{20,16},{24,20},{28,24},{1,29},{... | collective-permute-start | bytes 4616 | tf_op jit(solution)/shard_map/ppermute | solution.py:21
  265.8 7.6 %collective-permute-start.36 = (f32[2,6,32]{2,0,1:T(2,128)S(1)}, f32[2,6,32]{2,0,1:T(2,128)S(1)}, u32[]{:S(2)}, u32[]{:S(2)}) collective-permute-start(f32[2,6,32]{2,0,1:T(2,128)S(1)} %get-tuple-element.29), channel_id=1, source_target_pairs={{0,24},{4,28},{8,0},{12,4},{16,8},{20,12},{24,16},{28,20},{1,25},{... | collective-permute-start | bytes 4616 | tf_op jit(solution)/shard_map/ppermute | solution.py:21
  266.7 6.7 %collective-permute-start.37 = (f32[2,6,32]{2,0,1:T(2,128)S(1)}, f32[2,6,32]{2,0,1:T(2,128)S(1)}, u32[]{:S(2)}, u32[]{:S(2)}) collective-permute-start(f32[2,6,32]{2,0,1:T(2,128)S(1)} %get-tuple-element.28), channel_id=1, source_target_pairs={{0,20},{4,24},{8,28},{12,0},{16,4},{20,8},{24,12},{28,16},{1,21},{... | collective-permute-start | bytes 4616 | tf_op jit(solution)/shard_map/ppermute | solution.py:21
  320.1 9.3 %collective-permute-start.38 = (f32[2,6,32]{2,0,1:T(2,128)S(1)}, f32[2,6,32]{2,0,1:T(2,128)S(1)}, u32[]{:S(2)}, u32[]{:S(2)}) collective-permute-start(f32[2,6,32]{2,0,1:T(2,128)S(1)} %get-tuple-element.27), channel_id=1, source_target_pairs={{0,12},{4,16},{8,20},{12,24},{16,28},{20,0},{24,4},{28,8},{1,13},{... | collective-permute-start | bytes 4616 | tf_op jit(solution)/shard_map/ppermute | solution.py:21
  322.7 13.8 %collective-permute-start.39 = (f32[2,6,32]{2,0,1:T(2,128)S(1)}, f32[2,6,32]{2,0,1:T(2,128)S(1)}, u32[]{:S(2)}, u32[]{:S(2)}) collective-permute-start(f32[2,6,32]{2,0,1:T(2,128)S(1)} %get-tuple-element.26), channel_id=1, source_target_pairs={{0,8},{4,12},{8,16},{12,20},{16,24},{20,28},{24,0},{28,4},{1,9},{5... | collective-permute-start | bytes 4616 | tf_op jit(solution)/shard_map/ppermute | solution.py:21
  323.8 12.6 %collective-permute-start.40 = (f32[2,6,32]{2,0,1:T(2,128)S(1)}, f32[2,6,32]{2,0,1:T(2,128)S(1)}, u32[]{:S(2)}, u32[]{:S(2)}) collective-permute-start(f32[2,6,32]{2,0,1:T(2,128)S(1)} %get-tuple-element.25), channel_id=1, source_target_pairs={{0,4},{4,8},{8,12},{12,16},{16,20},{20,24},{24,28},{28,0},{1,5},{5... | collective-permute-start | bytes 4616 | tf_op jit(solution)/shard_map/ppermute | solution.py:21
  325.3 11.1 %collective-permute-start.41 = (f32[2,6,32]{2,0,1:T(2,128)S(1)}, f32[2,6,32]{2,0,1:T(2,128)S(1)}, u32[]{:S(2)}, u32[]{:S(2)}) collective-permute-start(f32[2,6,32]{2,0,1:T(2,128)S(1)} %get-tuple-element.24), channel_id=1, source_target_pairs={{0,28},{4,0},{8,4},{12,8},{16,12},{20,16},{24,20},{28,24},{1,29},{... | collective-permute-start | bytes 4616 | tf_op jit(solution)/shard_map/ppermute | solution.py:21
  328.6 7.9 %collective-permute-start.42 = (f32[2,6,32]{2,0,1:T(2,128)S(1)}, f32[2,6,32]{2,0,1:T(2,128)S(1)}, u32[]{:S(2)}, u32[]{:S(2)}) collective-permute-start(f32[2,6,32]{2,0,1:T(2,128)S(1)} %get-tuple-element.23), channel_id=1, source_target_pairs={{0,24},{4,28},{8,0},{12,4},{16,8},{20,12},{24,16},{28,20},{1,25},{... | collective-permute-start | bytes 4616 | tf_op jit(solution)/shard_map/ppermute | solution.py:21
  329.5 7.0 %collective-permute-start.43 = (f32[2,6,32]{2,0,1:T(2,128)S(1)}, f32[2,6,32]{2,0,1:T(2,128)S(1)}, u32[]{:S(2)}, u32[]{:S(2)}) collective-permute-start(f32[2,6,32]{2,0,1:T(2,128)S(1)} %get-tuple-element.22), channel_id=1, source_target_pairs={{0,20},{4,24},{8,28},{12,0},{16,4},{20,8},{24,12},{28,16},{1,21},{... | collective-permute-start | bytes 4616 | tf_op jit(solution)/shard_map/ppermute | solution.py:21
  379.5 4.8 %collective-permute-start.44 = (f32[2,6,4,16]{3,2,0,1:T(4,128)S(1)}, f32[2,6,4,16]{3,2,0,1:T(4,128)S(1)}, u32[]{:S(2)}, u32[]{:S(2)}) collective-permute-start(f32[2,6,4,16]{3,2,0,1:T(4,128)S(1)} %get-tuple-element.6), channel_id=1, source_target_pairs={{0,28},{4,0},{8,4},{12,8},{16,12},{20,16},{24,20},{28,24},{1,29},{... | collective-permute-start | bytes 9224 | tf_op jit(solution)/shard_map/ppermute | solution.py:21
  381.9 6.5 %collective-permute-start.45 = (f32[2,6,4,16]{3,2,0,1:T(4,128)S(1)}, f32[2,6,4,16]{3,2,0,1:T(4,128)S(1)}, u32[]{:S(2)}, u32[]{:S(2)}) collective-permute-start(f32[2,6,4,16]{3,2,0,1:T(4,128)S(1)} %get-tuple-element.7), channel_id=1, source_target_pairs={{0,4},{4,8},{8,12},{12,16},{16,20},{20,24},{24,28},{28,0},{1,5},{5... | collective-permute-start | bytes 9224 | tf_op jit(solution)/shard_map/ppermute | solution.py:21
  (44 other events, 89.1 us)
where the time goes:
time: 391 us
  local copies, waits for them, and re-layouts  259 us (66%)
  starting transfers between devices  76.1 us (19%)
  blocking collectives  37.5 us (10%)
  waiting for transfers between devices  7.43 us (2%)
  matrix products  6.04 us (2%)
    gather x72, local copies, waits for them, and re-layouts, body(): jnp.take(extended, neighbours[slot_index], axis=2)  236 us
    ppermute x46, starting transfers between devices, shifted(): return lax.ppermute(value, axis, pairs)  76.1 us
    all_gather x6, blocking collectives, body(): gathered = lax.all_gather(correction, 'inst', axis=0, tiled=True)  37.5 us
  transfers between devices with their start and end apart: 46, of which 5 were waited for; matrix products, arithmetic and copies ran while one was open for 0% of the time, Pallas kernels for 0%

commit v1 on v0

v1 whole, which is shorter than its diff:
```python
import jax
import jax.numpy as jnp
import numpy as np
from jax import lax
from jax.experimental import pallas as pl
from jax.experimental.pallas import tpu as pltpu
from jax.sharding import PartitionSpec as P

INST = 8
HB_INST = 7
AGG = 8
BLK = 128
RAD = 3
ITERS = 6
LANES = 128
MIB = 1024 * 1024

CBLK = BLK // AGG
PER_TILE = LANES // CBLK
OFFSETS = [slot - RAD if slot < RAD else slot - RAD + 1 for slot in range(2 * RAD)]


def fourier_basis():
    points = 2.0 * np.pi * np.arange(HB_INST) / HB_INST
    basis = np.zeros((INST, INST))
    basis[0, :HB_INST] = 1.0 / np.sqrt(HB_INST)
    for wave in range(1, INST // 2):
        basis[2 * wave, :HB_INST] = np.sqrt(2.0 / HB_INST) * np.cos(wave * points)
        basis[2 * wave + 1, :HB_INST] = np.sqrt(2.0 / HB_INST) * np.sin(wave * points)
    return basis.astype(np.float32)


def halves(value):
    high = value.astype(jnp.bfloat16)
    low = (value - high.astype(jnp.float32)).astype(jnp.bfloat16)
    return high, low


def stacked(value):
    return jnp.concatenate(halves(value), axis=0)


def dot(lhs, rhs):
    return jnp.dot(lhs, rhs, preferred_element_type=jnp.float32)


def dot_nt(lhs, rhs):
    return lax.dot_general(lhs, rhs, (((1,), (1,)), ((), ())), preferred_element_type=jnp.float32)


def block_order(routes_ref, order_ref, partition, n_cell):
    blocks = routes_ref.shape[1]
    handed = blocks // 16
    above = jnp.where(partition + 1 == n_cell, 0, partition + 1)

    def place(block, heads):
        first, own, last = heads
        route = routes_ref[0, block]
        is_own = route == partition
        is_above = route == above
        position = jnp.where(is_own, own, jnp.where(is_above, first, last))
        position = jnp.minimum(position, blocks - 1)
        order_ref[0, position] = block
        one = jnp.int32(1)
        zero = jnp.int32(0)
        return (
            first + jnp.where(is_above, one, zero),
            own + jnp.where(is_own, one, zero),
            last + jnp.where(is_own | is_above, zero, one),
        )

    lax.fori_loop(0, blocks, place, (jnp.int32(0), jnp.int32(handed), jnp.int32(blocks - handed)))


def restrict_kernel(n_cell, index_ref, routes_ref, lists_ref, fine_ref, map_ref, own_ref, send_ref, order_ref, flat_ref):
    partition = index_ref[0]
    var_count, inst_dev, _ = fine_ref.shape
    blocks = map_ref.shape[0]
    rows = var_count * inst_dev
    for var in range(var_count):
        flat_ref[var * inst_dev : (var + 1) * inst_dev, :] = fine_ref[var]
    flat_ref[rows:, :] = jnp.zeros((flat_ref.shape[0] - rows, flat_ref.shape[1]), jnp.float32)
    block_order(routes_ref, order_ref, partition, n_cell)
    height = flat_ref.shape[0]
    coarse_ids = lax.broadcasted_iota(jnp.int32, (LANES, BLK), 0)
    for tile in range(blocks // PER_TILE):
        total = jnp.zeros((2 * height, LANES), jnp.float32)
        for pair in range(PER_TILE // 2):
            values = []
            hots = []
            for place in (2 * pair, 2 * pair + 1):
                block = order_ref[0, tile * PER_TILE + place]
                values.append(flat_ref[:, pl.ds(pl.multiple_of(block * BLK, BLK), BLK)])
                target = map_ref[pl.ds(block, 1), :] + place * CBLK
                hots.append(jnp.where(coarse_ids == target, 1.0, 0.0).astype(jnp.bfloat16))
            total = total + dot_nt(stacked(jnp.concatenate(values, axis=1)), jnp.concatenate(hots, axis=1))
        own_ref[:, tile * LANES : (tile + 1) * LANES] = total[:height] + total[height:]
    lane = lax.broadcasted_iota(jnp.int32, (height, LANES), 1)
    edge = blocks // 16 * CBLK
    both = jnp.where(lane < edge, own_ref[:, :LANES], own_ref[:, own_ref.shape[1] - LANES :])
    width = send_ref.shape[2]
    lists = lists_ref[...].astype(jnp.float32)
    lists = jnp.concatenate([lists, jnp.zeros((1, width - lists.shape[1]), jnp.float32)], axis=1)
    row = lax.broadcasted_iota(jnp.int32, (height, width), 0)
    wide = jnp.concatenate([both, jnp.zeros((height, width - LANES), jnp.float32)], axis=1)
    message = jnp.where(row == rows, lists, wide)
    for target in range(n_cell):
        send_ref[target] = message


def arrive_kernel(n_cell, rows, share, index_ref, got_ref, own_ref, out_ref, pack_ref):
    partition = index_ref[0]
    below = jnp.where(partition == 0, n_cell - 1, partition - 1)
    above = jnp.where(partition + 1 == n_cell, 0, partition + 1)
    height, coarse_dev = own_ref.shape
    edge = coarse_dev // 16
    lane = lax.broadcasted_iota(jnp.int32, (height, LANES), 1)
    row = lax.broadcasted_iota(jnp.int32, (height, LANES), 0)
    first = got_ref[below][:, :LANES]
    last = got_ref[above][:, :LANES]
    out_ref[...] = own_ref[...]
    out_ref[:, :LANES] = jnp.where(row < rows, jnp.where(lane < edge, first, own_ref[:, :LANES]), 0.0)
    tail = own_ref[:, coarse_dev - LANES :]
    out_ref[:, coarse_dev - LANES :] = jnp.where(row < rows, jnp.where(lane >= LANES - edge, last, tail), 0.0)
    width = pack_ref.shape[1]
    lane = lax.broadcasted_iota(jnp.int32, (1, width), 1)
    listed = jnp.full((1, width), -1.0, jnp.float32)
    for slot, offset in enumerate(OFFSETS):
        receiver = lax.rem(partition - offset + n_cell, n_cell)
        from_receiver = got_ref[receiver][rows : rows + 1, :]
        inside = (lane >= slot * share) & (lane < (slot + 1) * share)
        listed = jnp.where(inside, from_receiver, listed)
    listed = listed.astype(jnp.int32)
    ids = lax.broadcasted_iota(jnp.int32, (coarse_dev, width), 0)
    pack_ref[...] = jnp.where(ids == listed, 1.0, 0.0).astype(jnp.bfloat16)


def matrix_kernel(neighbours_ref, weights_ref, high_ref, low_ref):
    slots, coarse_dev = neighbours_ref.shape
    step = 64
    for tile in range(coarse_dev // LANES):
        span = slice(tile * LANES, (tile + 1) * LANES)
        ids = neighbours_ref[:, span]
        weights = weights_ref[:, span]

        def chunk(block, carry):
            base = pl.multiple_of(block * step, step)
            rows = lax.broadcasted_iota(jnp.int32, (step, LANES), 0) + base
            total = jnp.zeros((step, LANES), jnp.float32)
            for slot in range(slots):
                total = total + jnp.where(rows == ids[slot : slot + 1], weights[slot : slot + 1], 0.0)
            high, low = halves(total)
            high_ref[pl.ds(base, step), span] = high
            low_ref[pl.ds(base, step), span] = low
            return carry

        lax.fori_loop(0, high_ref.shape[0] // step, chunk, 0)


def swap_pairs(value):
    height = value.shape[0]
    row = lax.broadcasted_iota(jnp.int32, value.shape, 0)
    return jnp.where(row % 2 == 0, pltpu.roll(value, height - 1, 0), pltpu.roll(value, 1, 0))


def by_parity(shape, even, odd):
    row = lax.broadcasted_iota(jnp.int32, shape, 0)
    return jnp.where(row % 2 == 0, even, odd)


def pack_halo(value, pack_ref):
    packed = dot(stacked(value), pack_ref[...])
    return packed[: value.shape[0]] + packed[value.shape[0] :]


def begin_kernel(index_ref, basis_ref, gathered_ref, weights_ref, spectral_ref, extra_ref, pack_ref,
                 start_ref, inverse_ref, coupled_ref, send_ref, diag_ref):
    pair = index_ref[1]
    groups, height, coarse_dev = gathered_ref.shape
    var_count = extra_ref.shape[0]
    value = jnp.zeros((height, coarse_dev), jnp.float32)
    shape = (height, coarse_dev)
    for group in range(groups):
        part = gathered_ref[group]
        straight = by_parity(shape, basis_ref[2 * pair, 2 * group], basis_ref[2 * pair + 1, 2 * group + 1])
        crossed = by_parity(shape, basis_ref[2 * pair, 2 * group + 1], basis_ref[2 * pair + 1, 2 * group])
        value = value + straight * part + crossed * swap_pairs(part)
    spectral = spectral_ref[...]
    shared = jnp.sum(weights_ref[...], axis=0, keepdims=True) + 3.0 * spectral
    diag_ref[...] = jnp.ones(shape, jnp.float32)
    for var in range(var_count):
        diag_ref[2 * var : 2 * var + 2, :] = jnp.broadcast_to(shared + extra_ref[var : var + 1, :], (2, coarse_dev))
    inverse = 1.0 / diag_ref[...]
    wave = pair.astype(jnp.float32)
    start = value * inverse
    start_ref[...] = start
    inverse_ref[...] = inverse
    coupled_ref[...] = by_parity(shape, wave, -wave) * spectral * inverse
    send = pack_halo(start, pack_ref)
    for target in range(send_ref.shape[0]):
        send_ref[target] = send


def new_correction(share, partition, got_ref, value, start_ref, inverse_ref, coupled_ref, high_ref, low_ref):
    n_cell, height, width = got_ref.shape
    coarse_dev = value.shape[1]
    lane = lax.broadcasted_iota(jnp.int32, (height, width), 1)
    halo = jnp.zeros((height, width), jnp.float32)
    for slot, offset in enumerate(OFFSETS):
        sender = lax.rem(partition + offset + n_cell, n_cell)
        inside = (lane >= slot * share) & (lane < (slot + 1) * share)
        halo = jnp.where(inside, got_ref[sender], halo)
    extended = stacked(jnp.concatenate([value, halo], axis=1))
    both = dot(extended, high_ref[...])
    total = both[:height] + both[height:] + dot(extended[:height], low_ref[...])
    return start_ref[...] + total * inverse_ref[...] - coupled_ref[...] * swap_pairs(value)


def sweep_kernel(share, index_ref, got_ref, value_ref, start_ref, inverse_ref, coupled_ref, high_ref, low_ref, pack_ref,
                 out_ref, send_ref):
    value = new_correction(
        share, index_ref[0], got_ref, value_ref[...], start_ref, inverse_ref, coupled_ref, high_ref, low_ref
    )
    out_ref[...] = value
    send = pack_halo(value, pack_ref)
    for target in range(send_ref.shape[0]):
        send_ref[target] = send


def last_kernel(share, index_ref, got_ref, value_ref, start_ref, inverse_ref, coupled_ref, high_ref, low_ref,
                out_ref, first_ref, last_ref):
    value = new_correction(
        share, index_ref[0], got_ref, value_ref[...], start_ref, inverse_ref, coupled_ref, high_ref, low_ref
    )
    out_ref[...] = value
    first_ref[...] = value[:, :LANES]
    last_ref[...] = value[:, value.shape[1] - LANES :]


def finish_kernel(index_ref, basis_ref, order_ref, gathered_ref, map_ref, coarse_ref, fine_ref, flat_ref):
    pair = index_ref[1]
    var_count, inst_dev, coarse_dev = coarse_ref.shape
    groups, height, wide = gathered_ref.shape
    blocks = map_ref.shape[0]
    edge = blocks // 16 * CBLK
    value = jnp.zeros((height, wide), jnp.float32)
    shape = (height, wide)
    for group in range(groups):
        part = gathered_ref[group]
        straight = by_parity(shape, basis_ref[2 * group, 2 * pair], basis_ref[2 * group + 1, 2 * pair + 1])
        crossed = by_parity(shape, basis_ref[2 * group + 1, 2 * pair], basis_ref[2 * group, 2 * pair + 1])
        value = value + straight * part + crossed * swap_pairs(part)
    for var in range(var_count):
        coarse_ref[var] = value[inst_dev * var : inst_dev * (var + 1), :coarse_dev]
    lane = lax.broadcasted_iota(jnp.int32, (height, LANES), 1)
    first_back = value[:, coarse_dev + LANES : coarse_dev + 2 * LANES]
    last_back = value[:, coarse_dev : coarse_dev + LANES]
    coarse_ids = lax.broadcasted_iota(jnp.int32, (LANES, BLK), 0)
    tiles = blocks // PER_TILE
    for tile in range(tiles):
        part = value[:, tile * LANES : (tile + 1) * LANES]
        if tile == 0:
            part = jnp.where(lane < edge, last_back, part)
        if tile == tiles - 1:
            part = jnp.where(lane >= LANES - edge, first_back, part)
        part = stacked(part)
        for pair_id in range(PER_TILE // 2):
            hots = []
            spots = []
            for place in (2 * pair_id, 2 * pair_id + 1):
                block = order_ref[0, tile * PER_TILE + place]
                target = map_ref[pl.ds(block, 1), :] + place * CBLK
                hots.append(jnp.where(coarse_ids == target, 1.0, 0.0).astype(jnp.bfloat16))
                spots.append(block)
            both = dot(part, jnp.concatenate(hots, axis=1))
            both = both[:height] + both[height:]
            for place, block in enumerate(spots):
                span = pl.ds(pl.multiple_of(block * BLK, BLK), BLK)
                flat_ref[:, span] = both[:, place * BLK : (place + 1) * BLK]
    for var in range(var_count):
        fine_ref[var] = flat_ref[inst_dev * var : inst_dev * (var + 1), :]


SMEM = pl.BlockSpec(memory_space=pltpu.SMEM)
VMEM = pl.BlockSpec(memory_space=pltpu.VMEM)


def call(kernel, outs, name, in_smem, n_in, out_smem=(), scratch=(), limit=16):
    return pl.pallas_call(
        kernel,
        name=name,
        out_shape=outs,
        in_specs=[SMEM if at in in_smem else VMEM for at in range(n_in)],
        out_specs=[SMEM if at in out_smem else VMEM for at in range(len(outs))],
        scratch_shapes=list(scratch),
        compiler_params=pltpu.CompilerParams(vmem_limit_bytes=limit * MIB),
    )


def shifted(value, axis, steps):
    count = lax.axis_size(axis)
    pairs = [(source, (source + steps) % count) for source in range(count)]
    return lax.ppermute(value, axis, pairs)


def f32(*shape):
    return jax.ShapeDtypeStruct(shape, jnp.float32)


def body(fine_residual, fine_map, routes, receive_lists, neighbours, face_weights, spectral_coef, diag_extra):
    n_cell = lax.axis_size("cell")
    inst_dev, var_count, fine_dev = fine_residual.shape
    blocks = routes.shape[1]
    coarse_dev = blocks * CBLK
    rows = inst_dev * var_count
    height = -(-(rows + 1) // 16) * 16
    halo = receive_lists.shape[1]
    halo_pad = -(-halo // 256) * 256
    share = halo // (2 * RAD)
    index = jnp.stack([lax.axis_index("cell"), lax.axis_index("inst")]).astype(jnp.int32)
    basis = jnp.asarray(fourier_basis())
    cell_map = fine_map.reshape(blocks, BLK)
    fine = fine_residual.transpose(1, 0, 2)
    spectral = spectral_coef.reshape(1, coarse_dev)

    own, send, order = call(
        lambda *refs: restrict_kernel(n_cell, *refs),
        [f32(height, coarse_dev), f32(n_cell, height, halo_pad), jax.ShapeDtypeStruct((1, blocks), jnp.int32)],
        "restrict", (0, 1), 5, (2,), [pltpu.VMEM((height, fine_dev), jnp.float32)],
    )(index, routes, receive_lists, fine, cell_map)
    got = lax.all_to_all(send, "cell", 0, 0)
    arrived, pack = call(
        lambda *refs: arrive_kernel(n_cell, rows, share, *refs),
        [f32(height, coarse_dev), jax.ShapeDtypeStruct((coarse_dev, halo_pad), jnp.bfloat16)],
        "arrive", (0,), 3,
    )(index, got, own)
    gathered = lax.all_gather(arrived, "inst", axis=0)
    half = jax.ShapeDtypeStruct((coarse_dev + halo_pad, coarse_dev), jnp.bfloat16)
    high, low = call(matrix_kernel, [half, half], "matrix", (), 2)(neighbours, face_weights)
    state = f32(height, coarse_dev)
    message = f32(n_cell, height, halo_pad)
    start, inverse, coupled, send = call(
        begin_kernel, [state, state, state, message], "begin", (0, 1), 7, (),
        [pltpu.VMEM((height, coarse_dev), jnp.float32)],
    )(index, basis, gathered, face_weights, spectral, diag_extra, pack)
    value = start
    for sweep in range(ITERS - 1):
        got = lax.all_to_all(send, "cell", 0, 0)
        value, send = call(lambda *refs: sweep_kernel(share, *refs), [state, message], "sweep", (0,), 9)(
            index, got, value, start, inverse, coupled, high, low, pack
        )
    got = lax.all_to_all(send, "cell", 0, 0)
    value, first, last = call(lambda *refs: last_kernel(share, *refs), [state, f32(height, LANES), f32(height, LANES)], "last", (0,), 8)(
        index, got, value, start, inverse, coupled, high, low
    )
    last_back = shifted(first, "cell", -1)
    first_back = shifted(last, "cell", 1)
    joined = jnp.concatenate([value, last_back, first_back], axis=1)
    gathered = lax.all_gather(joined, "inst", axis=0)
    coarse, fine_out = call(
        finish_kernel, [f32(var_count, inst_dev, coarse_dev), f32(var_count, inst_dev, fine_dev)],
        "finish", (0, 1, 2), 5, (), [pltpu.VMEM((height, fine_dev), jnp.float32)],
    )(index, basis, order, gathered, cell_map)
    return fine_out.transpose(1, 0, 2), coarse.transpose(1, 0, 2)


def solution(mesh):
    in_specs = (
        P("inst", None, "cell"),
        P("cell"),
        P("cell", None),
        P("cell", None),
        P(None, "cell"),
        P(None, "cell"),
        P("cell"),
        P(None, "cell"),
    )
    out_specs = (P("inst", None, "cell"), P("inst", None, "cell"))
    return jax.shard_map(body, mesh=mesh, in_specs=in_specs, out_specs=out_specs, check_vma=False)
```

time: 391 us -> 123 us (0.31)
  local copies, waits for them, and re-layouts: 259 us -> 10.7 us
  starting transfers between devices: 76.1 us -> 5.41 us
  blocking collectives: 37.5 us -> 78.3 us
  Pallas kernels: 0 us -> 21.7 us
  matrix products: 6.04 us -> 0 us
    gather x85 -> x0, local copies, waits for them, and re-layouts: 243 us -> none  [the longest x72 236 us: body(): jnp.take(extended, neighbours[slot_index], axis=2)]
    ppermute x46 -> x2, starting transfers between devices: 76.1 us -> 2.03 us  [shifted(): return lax.ppermute(value, axis, pairs)]
    all_to_all x0 -> x6, blocking collectives: none -> 66.5 us  [body(): got = lax.all_to_all(send, 'cell', 0, 0)]
    all_gather x6 -> x2, blocking collectives: 37.5 us -> 11.9 us  [the longest x1 6.09 us: body(): gathered = lax.all_gather(joined, 'inst', axis=0)]
    pallas_call x0 -> x11, Pallas kernels: none -> 21.7 us  [the longest x5 8.03 us: body(): call(lambda *refs: sweep_kernel(share, *refs), [state, message], 'sweep',...]
    unnamed x124 -> x28, local copies, waits for them, and re-layouts: 0.93 us -> 10.7 us
    concatenate x14 -> x0, local copies, waits for them, and re-layouts: 7.67 us -> none  [the longest x12 7.42 us: body(): jnp.concatenate([correction, jnp.concatenate(pieces, axis=2)], axis=2)]
    dot_general x10 -> x0, matrix products: 6.04 us -> none  [the longest x6 3.33 us: body(): jnp.einsum('nm,mvc->nvc', spec_rows, gathered, precision=exact_precision)]
  transfers between devices with their start and end apart: 46 -> 3, of which waited for: 5 -> 2; matrix products, arithmetic and copies ran while one was open for 0% -> 0% of each run, Pallas kernels for 0% -> 4%
where the time goes in v1:
time: 123 us; the launch traced here: 122 us
  blocking collectives  78.3 us (64%)
  Pallas kernels  21.7 us (18%)
  local copies, waits for them, and re-layouts  10.7 us (9%)
  starting transfers between devices  5.41 us (4%)
  waiting for transfers between devices  5.4 us (4%)
    all_to_all x6, blocking collectives, body(): got = lax.all_to_all(send, 'cell', 0, 0)  66.5 us
    unnamed x28, local copies, waits for them, and re-layouts  10.7 us
    pallas_call x5, Pallas kernels, body(): call(lambda *refs: sweep_kernel(share, *refs), [state, message], 'sweep',...  8.03 us
    all_gather x1, blocking collectives, body(): gathered = lax.all_gather(joined, 'inst', axis=0)  6.09 us
    all_gather x1, blocking collectives, body(): gathered = lax.all_gather(arrived, 'inst', axis=0)  5.78 us
    ppermute x2, waiting for transfers between devices, shifted(): return lax.ppermute(value, axis, pairs)  5.39 us
    pallas_call x1, Pallas kernels, body(): call(matrix_kernel, [half, half], 'matrix', (), 2)(neighbours, face_weights)  5.07 us
    all_to_all x1, starting transfers between devices, body(): got = lax.all_to_all(send, 'cell', 0, 0)  3.37 us
  transfers between devices with their start and end apart: 3, of which 2 were waited for; matrix products, arithmetic and copies ran while one was open for 0% of the time, Pallas kernels for 4%

profile of v1, /device:TPU:0, one launch (start us, length us, event | category | flops | bytes accessed | tf_op | source)
XLA Modules:
  0.0 122.4 jit_solution(5762857904417321003)
XLA Ops:
  0.6 0.1 pad_add_fusion.refs_0_.index_ref
  0.7 0.0 copy-start.2
  0.7 1.0 copy-done.2
  1.7 0.0 copy-start.5
  1.7 0.8 copy-done.5
  2.5 0.0 copy-start.12
  2.5 0.7 copy-done.12
  3.1 0.0 copy-start.13
  3.1 0.7 copy-done.13
  3.8 2.8 %restrict.1 = (f32[16,1024]{1,0:T(8,128)S(1)}, f32[8,16,256]{2,1,0:T(8,128)S(1)}, s32[1,64]{1,0:T(1,128)S(1)}) custom-call(s32[2]{0:T(128)S(1)} %pad_add_fusion.refs_0_.index_ref, s32[1,64]{1,0:T(1,128)S(1)} %copy-done.13, s32[1,192]{1,0:T(1,128)S(1)} %copy-done.12, f32[6,2,8192]{2,1,0:T(2,128)S(1)} %bitcast.11, s32[64,128]{1,0:T(8,128)S(1)} %bitcast.12), custom_call_target="tpu_custom_call" | custom-call | tf_op jit(solution)/shard_map/restrict/pallas_call | solution.py:326
  6.6 14.5 %all_to_all.35.refs_1_ = f32[8,16,256]{2,1,0:T(8,128)S(1)} all-to-all(f32[8,16,256]{2,1,0:T(8,128)S(1)} %get-tuple-element.29), channel_id=1, replica_groups=mesh['cell'=8,'inst'=4] {'cell'}, dimensions={0} | all-to-all | bytes 262144 | tf_op jit(solution)/shard_map/all_to_all | solution.py:331
  21.0 0.7 arrive.1
  21.7 5.8 %all-gather = f32[64,1024]{1,0:T(8,128)S(1)} all-gather(f32[16,1024]{1,0:T(8,128)S(1)} %get-tuple-element.31), channel_id=2, replica_groups=mesh['cell'=8,'inst'=4] {'inst'}, dimensions={0}, use_global_device_ids=true | all-gather | bytes 327680 | tf_op jit(solution)/shard_map/all_gather | solution.py:337
  27.5 0.0 copy-start.3
  27.5 0.8 copy-done.3
  28.3 0.0 copy-start.7
  28.3 0.8 copy-done.7
  29.0 0.0 copy-start.9
  29.0 0.7 copy-done.9
  29.7 0.0 copy-start.11
  29.7 0.7 copy-done.11
  30.4 1.6 %begin.1 = (f32[16,1024]{1,0:T(8,128)S(1)}, f32[16,1024]{1,0:T(8,128)S(1)}, f32[16,1024]{1,0:T(8,128)S(1)}, f32[8,16,256]{2,1,0:T(8,128)}) custom-call(s32[2]{0:T(128)S(1)} %pad_add_fusion.refs_0_.index_ref, f32[8,8]{1,0:T(8,128)S(1)} %copy-done.9, f32[4,16,1024]{2,1,0:T(8,128)S(1)} %bitcast.10, f32[6,1024]{1,0:T(8,128)S(1)} %copy-done.3, ...), custom_call_target="tpu_custom_call" | custom-call | tf_op jit(solution)/shard_map/begin/pallas_call | solution.py:342
  31.9 3.4 %all-to-all-start.1 = ((f32[8,16,256]{2,1,0:T(8,128)}), f32[8,16,256]{2,1,0:T(8,128)S(1)}, u32[]{:S(2)}, u32[]{:S(2)}) async-start(f32[8,16,256]{2,1,0:T(8,128)} %get-tuple-element.33), calls=%async_computation.1 | async-start | bytes 262144 | tf_op jit(solution)/shard_map/all_to_all | solution.py:348
  35.3 0.0 copy-start.4
  35.3 0.7 copy-done.4
  36.1 0.0 copy-start.8
  36.1 0.8 copy-done.8
  36.8 5.1 %matrix.1 = (bf16[1280,1024]{1,0:T(8,128)(2,1)S(1)}, bf16[1280,1024]{1,0:T(8,128)(2,1)S(1)}) custom-call(s32[6,1024]{1,0:T(8,128)S(1)} %copy-done.8, f32[6,1024]{1,0:T(8,128)S(1)} %copy-done.4), custom_call_target="tpu_custom_call" | custom-call | tf_op jit(solution)/shard_map/matrix/pallas_call | solution.py:339
  41.9 0.0 copy-start
  41.9 1.5 %copy-done = bf16[1280,1024]{1,0:T(8,128)(2,1)} copy-done((bf16[1280,1024]{1,0:T(8,128)(2,1)}, bf16[1280,1024]{1,0:T(8,128)(2,1)S(1)}, u32[]{:S(2)}) %copy-start) | copy-done | bytes 2621464
  43.4 0.0 all-to-all-done.1.refs_1_
  43.4 0.0 copy-start.1
  43.4 1.7 %copy-done.1 = bf16[1280,1024]{1,0:T(8,128)(2,1)S(1)} copy-done((bf16[1280,1024]{1,0:T(8,128)(2,1)S(1)}, bf16[1280,1024]{1,0:T(8,128)(2,1)}, u32[]{:S(2)}) %copy-start.1) | copy-done | bytes 2621464
  45.2 1.6 %sweep.5 = (f32[16,1024]{1,0:T(8,128)S(1)}, f32[8,16,256]{2,1,0:T(8,128)S(1)}) custom-call(s32[2]{0:T(128)S(1)} %pad_add_fusion.refs_0_.index_ref, f32[8,16,256]{2,1,0:T(8,128)S(1)} %all-to-all-done.1.refs_1_, f32[16,1024]{1,0:T(8,128)S(1)} %get-tuple-element.34.refs_2_.refs_3_, f32[16,1024]{1,0:T(8,128)S(1)} %get-tuple-element.34.refs_2_.refs_3_, ...), custom_call_target="tpu_custom_call" | custom-call | tf_op jit(solution)/shard_map/sweep/pallas_call | solution.py:349
  46.8 13.1 %all_to_all.36.refs_1_ = f32[8,16,256]{2,1,0:T(8,128)S(1)} all-to-all(f32[8,16,256]{2,1,0:T(8,128)S(1)} %get-tuple-element.39), channel_id=1, replica_groups=mesh['cell'=8,'inst'=4] {'cell'}, dimensions={0} | all-to-all | bytes 262144 | tf_op jit(solution)/shard_map/all_to_all | solution.py:348
  59.9 1.6 %sweep.6 = (f32[16,1024]{1,0:T(8,128)S(1)}, f32[8,16,256]{2,1,0:T(8,128)S(1)}) custom-call(s32[2]{0:T(128)S(1)} %pad_add_fusion.refs_0_.index_ref, f32[8,16,256]{2,1,0:T(8,128)S(1)} %all_to_all.36.refs_1_, f32[16,1024]{1,0:T(8,128)S(1)} %get-tuple-element.40.refs_2_, f32[16,1024]{1,0:T(8,128)S(1)} %get-tuple-element.34.refs_2_.refs_3_, ...), custom_call_target="tpu_custom_call" | custom-call | tf_op jit(solution)/shard_map/sweep/pallas_call | solution.py:349
  61.5 9.7 %all_to_all.37.refs_1_ = f32[8,16,256]{2,1,0:T(8,128)S(1)} all-to-all(f32[8,16,256]{2,1,0:T(8,128)S(1)} %get-tuple-element.41), channel_id=1, replica_groups=mesh['cell'=8,'inst'=4] {'cell'}, dimensions={0} | all-to-all | bytes 262144 | tf_op jit(solution)/shard_map/all_to_all | solution.py:348
  71.2 1.6 %sweep.7 = (f32[16,1024]{1,0:T(8,128)S(1)}, f32[8,16,256]{2,1,0:T(8,128)S(1)}) custom-call(s32[2]{0:T(128)S(1)} %pad_add_fusion.refs_0_.index_ref, f32[8,16,256]{2,1,0:T(8,128)S(1)} %all_to_all.37.refs_1_, f32[16,1024]{1,0:T(8,128)S(1)} %get-tuple-element.42.refs_2_, f32[16,1024]{1,0:T(8,128)S(1)} %get-tuple-element.34.refs_2_.refs_3_, ...), custom_call_target="tpu_custom_call" | custom-call | tf_op jit(solution)/shard_map/sweep/pallas_call | solution.py:349
  72.8 9.7 %all_to_all.38.refs_1_ = f32[8,16,256]{2,1,0:T(8,128)S(1)} all-to-all(f32[8,16,256]{2,1,0:T(8,128)S(1)} %get-tuple-element.43), channel_id=1, replica_groups=mesh['cell'=8,'inst'=4] {'cell'}, dimensions={0} | all-to-all | bytes 262144 | tf_op jit(solution)/shard_map/all_to_all | solution.py:348
  82.6 1.6 %sweep.8 = (f32[16,1024]{1,0:T(8,128)S(1)}, f32[8,16,256]{2,1,0:T(8,128)S(1)}) custom-call(s32[2]{0:T(128)S(1)} %pad_add_fusion.refs_0_.index_ref, f32[8,16,256]{2,1,0:T(8,128)S(1)} %all_to_all.38.refs_1_, f32[16,1024]{1,0:T(8,128)S(1)} %get-tuple-element.44.refs_2_, f32[16,1024]{1,0:T(8,128)S(1)} %get-tuple-element.34.refs_2_.refs_3_, ...), custom_call_target="tpu_custom_call" | custom-call | tf_op jit(solution)/shard_map/sweep/pallas_call | solution.py:349
  84.2 9.7 %all_to_all.39.refs_1_ = f32[8,16,256]{2,1,0:T(8,128)S(1)} all-to-all(f32[8,16,256]{2,1,0:T(8,128)S(1)} %get-tuple-element.45), channel_id=1, replica_groups=mesh['cell'=8,'inst'=4] {'cell'}, dimensions={0} | all-to-all | bytes 262144 | tf_op jit(solution)/shard_map/all_to_all | solution.py:348
  93.9 1.6 %sweep.9 = (f32[16,1024]{1,0:T(8,128)S(1)}, f32[8,16,256]{2,1,0:T(8,128)S(1)}) custom-call(s32[2]{0:T(128)S(1)} %pad_add_fusion.refs_0_.index_ref, f32[8,16,256]{2,1,0:T(8,128)S(1)} %all_to_all.39.refs_1_, f32[16,1024]{1,0:T(8,128)S(1)} %get-tuple-element.46.refs_2_, f32[16,1024]{1,0:T(8,128)S(1)} %get-tuple-element.34.refs_2_.refs_3_, ...), custom_call_target="tpu_custom_call" | custom-call | tf_op jit(solution)/shard_map/sweep/pallas_call | solution.py:349
  95.5 9.7 %all_to_all.40.refs_1_ = f32[8,16,256]{2,1,0:T(8,128)S(1)} all-to-all(f32[8,16,256]{2,1,0:T(8,128)S(1)} %get-tuple-element.47), channel_id=1, replica_groups=mesh['cell'=8,'inst'=4] {'cell'}, dimensions={0} | all-to-all | bytes 262144 | tf_op jit(solution)/shard_map/all_to_all | solution.py:352
  105.3 0.0 copy-start.6
  105.3 0.0 copy-start.10
  105.3 1.4 %last.1 = (f32[16,1024]{1,0:T(8,128)S(1)}, f32[16,128]{1,0:T(8,128)S(1)}, f32[16,128]{1,0:T(8,128)S(1)}) custom-call(s32[2]{0:T(128)S(1)} %pad_add_fusion.refs_0_.index_ref, f32[8,16,256]{2,1,0:T(8,128)S(1)} %all_to_all.40.refs_1_, f32[16,1024]{1,0:T(8,128)S(1)} %get-tuple-element.48.refs_2_, f32[16,1024]{1,0:T(8,128)S(1)} %get-tuple-element.34.refs_2_.refs_3_, ...), custom_call_target="tpu_custom_call" | custom-call | tf_op jit(solution)/shard_map/last/pallas_call | solution.py:353
  106.7 1.1 collective-permute-start
  107.8 1.0 collective-permute-start.1
  108.7 1.6 %collective-permute-done = f32[16,128]{1,0:T(8,128)S(1)} collective-permute-done((f32[16,128]{1,0:T(8,128)S(1)}, f32[16,128]{1,0:T(8,128)S(1)}, u32[]{:S(2)}, u32[]{:S(2)}) %collective-permute-start) | collective-permute-done | bytes 8224 | tf_op jit(solution)/shard_map/ppermute | solution.py:303
  110.3 3.8 %collective-permute-done.1 = f32[16,128]{1,0:T(8,128)S(1)} collective-permute-done((f32[16,128]{1,0:T(8,128)S(1)}, f32[16,128]{1,0:T(8,128)S(1)}, u32[]{:S(2)}, u32[]{:S(2)}) %collective-permute-start.1) | collective-permute-done | bytes 8224 | tf_op jit(solution)/shard_map/ppermute | solution.py:303
  114.1 6.1 %all-gather.1 = f32[64,1280]{1,0:T(8,128)S(1)} all-gather(f32[16,1280]{1,0:T(8,128)S(1)} %pad_maximum_fusion), channel_id=3, replica_groups=mesh['cell'=8,'inst'=4] {'inst'}, dimensions={0}, use_global_device_ids=true | all-gather | bytes 409600 | tf_op jit(solution)/shard_map/all_gather | solution.py:359
  120.2 0.0 copy-done.6
  120.2 0.0 copy-done.10
  120.2 2.2 %finish.1 = (f32[6,2,1024]{2,1,0:T(2,128)}, f32[6,2,8192]{2,1,0:T(2,128)}) custom-call(s32[2]{0:T(128)S(1)} %pad_add_fusion.refs_0_.index_ref, f32[8,8]{1,0:T(8,128)S(1)} %copy-done.10, s32[1,64]{1,0:T(1,128)S(1)} %get-tuple-element.28.order_ref, f32[4,16,1280]{2,1,0:T(8,128)S(1)} %bitcast.9, s32[64,128]{1,0:T(8,128)S(1)} %bitcast.13), custom_call_target="tpu_custom_call" | custom-call | tf_op jit(solution)/shard_map/finish/pallas_call | solution.py:360
  (1 shorter events, 0.0 us)
Async XLA Ops:
  0.7 1.0 copy-start.2
  1.7 0.8 copy-start.5
  2.5 0.7 copy-start.12
  3.1 0.7 copy-start.13
  27.5 0.8 copy-start.3
  28.3 0.8 copy-start.7
  29.0 0.7 copy-start.9
  29.7 0.7 copy-start.11
  31.9 11.5 %all-to-all-start.1 = ((f32[8,16,256]{2,1,0:T(8,128)}), f32[8,16,256]{2,1,0:T(8,128)S(1)}, u32[]{:S(2)}, u32[]{:S(2)}) async-start(f32[8,16,256]{2,1,0:T(8,128)} %get-tuple-element.33), calls=%async_computation.1 | async-start | bytes 262144 | tf_op jit(solution)/shard_map/all_to_all | solution.py:348
  35.3 0.8 copy-start.4
  36.1 0.8 copy-start.8
  41.9 1.5 %copy-start = (bf16[1280,1024]{1,0:T(8,128)(2,1)}, bf16[1280,1024]{1,0:T(8,128)(2,1)S(1)}, u32[]{:S(2)}) copy-start(bf16[1280,1024]{1,0:T(8,128)(2,1)S(1)} %get-tuple-element.38.refs_7_) | copy-start | bytes 7864324
  43.4 1.7 %copy-start.1 = (bf16[1280,1024]{1,0:T(8,128)(2,1)S(1)}, bf16[1280,1024]{1,0:T(8,128)(2,1)}, u32[]{:S(2)}) copy-start(bf16[1280,1024]{1,0:T(8,128)(2,1)} %copy-done) | copy-start | bytes 7864324
  105.3 14.9 %copy-start.6 = (s32[8192]{0:T(1024)S(1)}, s32[8192]{0:T(1024)}, u32[]{:S(2)}) copy-start(s32[8192]{0:T(1024)} %param.10) | copy-start | bytes 98308
  105.3 14.9 %copy-start.10 = (f32[8,8]{1,0:T(8,128)S(1)}, f32[8,8]{1,0:T(8,128)}, u32[]{:S(2)}) copy-start(f32[8,8]{1,0:T(8,128)} %constant.11.clone.basis_ref) | copy-start | bytes 772
  106.7 3.7 %collective-permute-start = (f32[16,128]{1,0:T(8,128)S(1)}, f32[16,128]{1,0:T(8,128)S(1)}, u32[]{:S(2)}, u32[]{:S(2)}) collective-permute-start(f32[16,128]{1,0:T(8,128)S(1)} %get-tuple-element.50), channel_id=1, source_target_pairs={{0,28},{4,0},{8,4},{12,8},{16,12},{20,16},{24,20},{28,24},{1,29},{... | collective-permute-start | bytes 24584 | tf_op jit(solution)/shard_map/ppermute | solution.py:303
  107.8 6.3 %collective-permute-start.1 = (f32[16,128]{1,0:T(8,128)S(1)}, f32[16,128]{1,0:T(8,128)S(1)}, u32[]{:S(2)}, u32[]{:S(2)}) collective-permute-start(f32[16,128]{1,0:T(8,128)S(1)} %get-tuple-element.51), channel_id=1, source_target_pairs={{0,4},{4,8},{8,12},{12,16},{16,20},{20,24},{24,28},{28,0},{1,5},{5... | collective-permute-start | bytes 24584 | tf_op jit(solution)/shard_map/ppermute | solution.py:303

commit v2 on v1

--- a/solution.py
+++ b/solution.py
@@ -173,11 +173,42 @@
     return packed[: value.shape[0]] + packed[value.shape[0] :]
 
 
-def begin_kernel(index_ref, basis_ref, gathered_ref, weights_ref, spectral_ref, extra_ref, pack_ref,
-                 start_ref, inverse_ref, coupled_ref, send_ref, diag_ref):
+def prepare_kernel(neighbours_ref, weights_ref, spectral_ref, extra_ref,
+                   high_ref, low_ref, inverse_ref, coupled_ref, topology_ref):
+    matrix_kernel(neighbours_ref, weights_ref, high_ref, low_ref)
+    slots, coarse_dev = neighbours_ref.shape
+    var_count = extra_ref.shape[0]
+    weights = weights_ref[...]
+    spectral = spectral_ref[...]
+    diagonal = jnp.sum(weights, axis=0, keepdims=True) + 3.0 * spectral + extra_ref[...]
+    inverse = 1.0 / diagonal
+    inverse_ref[...] = jnp.ones(inverse_ref.shape, jnp.float32)
+    for var in range(var_count):
+        inverse_ref[2 * var : 2 * var + 2, :] = jnp.broadcast_to(inverse[var : var + 1], (2, coarse_dev))
+    coupled_ref[...] = by_parity(coupled_ref.shape, spectral, -spectral) * inverse_ref[...]
+    topology_ref[...] = jnp.zeros(topology_ref.shape, jnp.float32)
+    topology_ref[0:slots, :] = neighbours_ref[...].astype(jnp.float32)
+    topology_ref[8 : 8 + slots, :] = weights
+    topology_ref[16 : 16 + var_count, :] = inverse
+
+
+def times(value, high, low):
+    height = value.shape[0]
+    extended = stacked(value)
+    both = dot(extended, high)
+    return both[:height] + both[height:] + dot(extended[:height], low)
+
+
+def local_part(value, start_ref, inverse_ref, coupled_ref, wave, high_ref, low_ref):
+    coarse_dev = value.shape[1]
+    total = times(value, high_ref[:coarse_dev], low_ref[:coarse_dev])
+    return start_ref[...] + total * inverse_ref[...] - wave * coupled_ref[...] * swap_pairs(value)
+
+
+def begin_kernel(index_ref, basis_ref, gathered_ref, inverse_ref, coupled_ref, topology_ref, pack_ref, high_ref, low_ref,
+                 start_ref, local_ref, send_ref):
     pair = index_ref[1]
     groups, height, coarse_dev = gathered_ref.shape
-    var_count = extra_ref.shape[0]
     value = jnp.zeros((height, coarse_dev), jnp.float32)
     shape = (height, coarse_dev)
     for group in range(groups):
@@ -185,56 +216,86 @@
         straight = by_parity(shape, basis_ref[2 * pair, 2 * group], basis_ref[2 * pair + 1, 2 * group + 1])
         crossed = by_parity(shape, basis_ref[2 * pair, 2 * group + 1], basis_ref[2 * pair + 1, 2 * group])
         value = value + straight * part + crossed * swap_pairs(part)
-    spectral = spectral_ref[...]
-    shared = jnp.sum(weights_ref[...], axis=0, keepdims=True) + 3.0 * spectral
-    diag_ref[...] = jnp.ones(shape, jnp.float32)
-    for var in range(var_count):
-        diag_ref[2 * var : 2 * var + 2, :] = jnp.broadcast_to(shared + extra_ref[var : var + 1, :], (2, coarse_dev))
-    inverse = 1.0 / diag_ref[...]
-    wave = pair.astype(jnp.float32)
-    start = value * inverse
+    start = value * inverse_ref[...]
     start_ref[...] = start
-    inverse_ref[...] = inverse
-    coupled_ref[...] = by_parity(shape, wave, -wave) * spectral * inverse
-    send = pack_halo(start, pack_ref)
+    local = local_part(start, start_ref, inverse_ref, coupled_ref, pair.astype(jnp.float32), high_ref, low_ref)
+    local_ref[...] = local
+    send = pack_halo(jnp.concatenate([start, local, topology_ref[...]], axis=0), pack_ref)
     for target in range(send_ref.shape[0]):
         send_ref[target] = send
 
 
-def new_correction(share, partition, got_ref, value, start_ref, inverse_ref, coupled_ref, high_ref, low_ref):
-    n_cell, height, width = got_ref.shape
-    coarse_dev = value.shape[1]
+def halo_of(partition, share, got_ref, top, height):
+    n_cell, _, width = got_ref.shape
     lane = lax.broadcasted_iota(jnp.int32, (height, width), 1)
     halo = jnp.zeros((height, width), jnp.float32)
     for slot, offset in enumerate(OFFSETS):
         sender = lax.rem(partition + offset + n_cell, n_cell)
         inside = (lane >= slot * share) & (lane < (slot + 1) * share)
-        halo = jnp.where(inside, got_ref[sender], halo)
-    extended = stacked(jnp.concatenate([value, halo], axis=1))
-    both = dot(extended, high_ref[...])
-    total = both[:height] + both[height:] + dot(extended[:height], low_ref[...])
-    return start_ref[...] + total * inverse_ref[...] - coupled_ref[...] * swap_pairs(value)
-
-
-def sweep_kernel(share, index_ref, got_ref, value_ref, start_ref, inverse_ref, coupled_ref, high_ref, low_ref, pack_ref,
-                 out_ref, send_ref):
-    value = new_correction(
-        share, index_ref[0], got_ref, value_ref[...], start_ref, inverse_ref, coupled_ref, high_ref, low_ref
+        halo = jnp.where(inside, got_ref[sender, top : top + height, :], halo)
+    return halo
+
+
+def double_kernel(share, first, last, slots, var_count, *refs):
+    refs = list(refs)
+    index_ref, got_ref, local_ref, start_ref, inverse_ref, coupled_ref, high_ref, low_ref, pack_ref = refs[:9]
+    refs = refs[9:]
+    if first:
+        edge_ref = None
+        halo_inverse_ref = None
+    else:
+        edge_ref, halo_inverse_ref = refs[:2]
+        refs = refs[2:]
+    partition = index_ref[0]
+    wave = index_ref[1].astype(jnp.float32)
+    n_cell, _, width = got_ref.shape
+    height, coarse_dev = local_ref.shape
+    out_refs = refs
+    if first:
+        out_refs, (edge_ref, halo_inverse_ref) = refs[:-2], refs[-2:]
+        told = halo_of(partition, share, got_ref, 2 * height, 24)
+        ids = told[:slots].astype(jnp.int32) - coarse_dev
+        weights = told[8 : 8 + slots]
+        rows = lax.broadcasted_iota(jnp.int32, (width, width), 0)
+        edge = jnp.zeros((width, width), jnp.float32)
+        for slot in range(slots):
+            edge = edge + jnp.where(rows == ids[slot : slot + 1], weights[slot : slot + 1], 0.0)
+        high, low = halves(edge)
+        edge_ref[0] = high
+        edge_ref[1] = low
+        halo_inverse_ref[...] = jnp.zeros((height, width), jnp.float32)
+        for var in range(var_count):
+            halo_inverse_ref[2 * var : 2 * var + 2, :] = jnp.broadcast_to(told[16 + var : 17 + var], (2, width))
+    halo_high = high_ref[coarse_dev:]
+    halo_low = low_ref[coarse_dev:]
+    lane = lax.broadcasted_iota(jnp.int32, (height, width), 1)
+    share_of = []
+    for offset in OFFSETS:
+        share_of.append(halo_of(lax.rem(partition + offset + n_cell, n_cell), share, got_ref, 0, height))
+    spread = times(jnp.concatenate(share_of, axis=0), edge_ref[0], edge_ref[1])
+    edge_total = jnp.zeros((height, width), jnp.float32)
+    for slot in range(len(OFFSETS)):
+        inside = (lane >= slot * share) & (lane < (slot + 1) * share)
+        edge_total = jnp.where(inside, spread[slot * height : (slot + 1) * height], edge_total)
+    next_halo = halo_of(partition, share, got_ref, height, height) + halo_inverse_ref[...] * edge_total
+    both = times(
+        jnp.concatenate([halo_of(partition, share, got_ref, 0, height), next_halo], axis=0), halo_high, halo_low
     )
-    out_ref[...] = value
-    send = pack_halo(value, pack_ref)
-    for target in range(send_ref.shape[0]):
+    value = local_ref[...] + both[:height] * inverse_ref[...]
+    local = local_part(value, start_ref, inverse_ref, coupled_ref, wave, high_ref, low_ref)
+    value = local + both[height:] * inverse_ref[...]
+    if last:
+        out_ref, first_ref, last_ref = out_refs
+        out_ref[...] = value
+        first_ref[...] = value[:, :LANES]
+        last_ref[...] = value[:, coarse_dev - LANES :]
+        return
+    out_ref, send_ref = out_refs
+    local = local_part(value, start_ref, inverse_ref, coupled_ref, wave, high_ref, low_ref)
+    out_ref[...] = local
+    send = pack_halo(jnp.concatenate([value, local], axis=0), pack_ref)
+    for target in range(n_cell):
         send_ref[target] = send
-
-
-def last_kernel(share, index_ref, got_ref, value_ref, start_ref, inverse_ref, coupled_ref, high_ref, low_ref,
-                out_ref, first_ref, last_ref):
-    value = new_correction(
-        share, index_ref[0], got_ref, value_ref[...], start_ref, inverse_ref, coupled_ref, high_ref, low_ref
-    )
-    out_ref[...] = value
-    first_ref[...] = value[:, :LANES]
-    last_ref[...] = value[:, value.shape[1] - LANES :]
 
 
 def finish_kernel(index_ref, basis_ref, order_ref, gathered_ref, map_ref, coarse_ref, fine_ref, flat_ref):
@@ -335,24 +396,38 @@
         "arrive", (0,), 3,
     )(index, got, own)
     gathered = lax.all_gather(arrived, "inst", axis=0)
+    slots = neighbours.shape[0]
     half = jax.ShapeDtypeStruct((coarse_dev + halo_pad, coarse_dev), jnp.bfloat16)
-    high, low = call(matrix_kernel, [half, half], "matrix", (), 2)(neighbours, face_weights)
     state = f32(height, coarse_dev)
-    message = f32(n_cell, height, halo_pad)
-    start, inverse, coupled, send = call(
-        begin_kernel, [state, state, state, message], "begin", (0, 1), 7, (),
-        [pltpu.VMEM((height, coarse_dev), jnp.float32)],
-    )(index, basis, gathered, face_weights, spectral, diag_extra, pack)
-    value = start
-    for sweep in range(ITERS - 1):
+    high, low, inverse, coupled, topology = call(
+        prepare_kernel, [half, half, state, state, f32(24, coarse_dev)], "prepare", (), 4
+    )(neighbours, face_weights, spectral, diag_extra)
+    start, local, send = call(
+        begin_kernel, [state, state, f32(n_cell, 2 * height + 24, halo_pad)], "begin", (0, 1), 9
+    )(index, basis, gathered, inverse, coupled, topology, pack, high, low)
+    edges = []
+    for pair in range(ITERS // 2):
         got = lax.all_to_all(send, "cell", 0, 0)
-        value, send = call(lambda *refs: sweep_kernel(share, *refs), [state, message], "sweep", (0,), 9)(
-            index, got, value, start, inverse, coupled, high, low, pack
-        )
-    got = lax.all_to_all(send, "cell", 0, 0)
-    value, first, last = call(lambda *refs: last_kernel(share, *refs), [state, f32(height, LANES), f32(height, LANES)], "last", (0,), 8)(
-        index, got, value, start, inverse, coupled, high, low
-    )
+        is_first = pair == 0
+        is_last = pair == ITERS // 2 - 1
+        outs = [state, f32(n_cell, 2 * height, halo_pad)]
+        if is_last:
+            outs = [state, f32(height, LANES), f32(height, LANES)]
+        if is_first:
+            outs += [jax.ShapeDtypeStruct((2, halo_pad, halo_pad), jnp.bfloat16), f32(height, halo_pad)]
+        outs = call(
+            lambda *refs: double_kernel(share, is_first, is_last, slots, var_count, *refs),
+            outs, "double", (0,), 9 + len(edges),
+        )(index, got, local, start, inverse, coupled, high, low, pack, *edges)
+        if is_first:
+            edges = outs[-2:]
+            outs = outs[:-2]
+        local, *rest = outs
+        if is_last:
+            first, last = rest
+        else:
+            (send,) = rest
+    value = local
     last_back = shifted(first, "cell", -1)
     first_back = shifted(last, "cell", 1)
     joined = jnp.concatenate([value, last_back, first_back], axis=1)

time: 123 us -> 103 us (0.84)
  blocking collectives: 78.3 us -> 55.6 us
  starting transfers between devices: 5.41 us -> 9.66 us
  Pallas kernels: 21.7 us -> 19.5 us
    all_to_all x6 -> x3, blocking collectives: 66.5 us -> 43.8 us  [body(): got = lax.all_to_all(send, 'cell', 0, 0)]
    all_to_all x1, starting transfers between devices: 3.37 us -> 7.32 us  [body(): got = lax.all_to_all(send, 'cell', 0, 0)]
    pallas_call x8 -> x5, Pallas kernels: 16.1 us -> 13.5 us  [the longest x3 6.84 us: body(): call(lambda *refs: double_kernel(share, is_first, is_last, slots, var_cou...]
    unnamed x28 -> x24, local copies, waits for them, and re-layouts: 10.7 us -> 9.96 us
  transfers between devices with their start and end apart: 3 -> 3, of which waited for: 2 -> 2; matrix products, arithmetic and copies ran while one was open for 0% -> 0% of each run, Pallas kernels for 4% -> 5%
where the time goes in v2:
time: 103 us; the launch traced here: 102 us
  blocking collectives  55.6 us (54%)
  Pallas kernels  19.5 us (19%)
  local copies, waits for them, and re-layouts  9.96 us (10%)
  starting transfers between devices  9.66 us (9%)
  waiting for transfers between devices  6.35 us (6%)
    all_to_all x3, blocking collectives, body(): got = lax.all_to_all(send, 'cell', 0, 0)  43.8 us
    unnamed x24, local copies, waits for them, and re-layouts  9.96 us
    all_to_all x1, starting transfers between devices, body(): got = lax.all_to_all(send, 'cell', 0, 0)  7.32 us
    pallas_call x3, Pallas kernels, body(): call(lambda *refs: double_kernel(share, is_first, is_last, slots, var_cou...  6.84 us
    ppermute x2, waiting for transfers between devices, shifted(): return lax.ppermute(value, axis, pairs)  6.34 us
    all_gather x1, blocking collectives, body(): gathered = lax.all_gather(joined, 'inst', axis=0)  6.09 us
    all_gather x1, blocking collectives, body(): gathered = lax.all_gather(arrived, 'inst', axis=0)  5.78 us
    pallas_call x1, Pallas kernels, body(): call(prepare_kernel, [half, half, state, state, f32(24, coarse_dev)], 'pr...  5.1 us
  transfers between devices with their start and end apart: 3, of which 2 were waited for; matrix products, arithmetic and copies ran while one was open for 0% of the time, Pallas kernels for 5%

profile of v2, /device:TPU:0, one launch (start us, length us, event | category | flops | bytes accessed | tf_op | source)
XLA Modules:
  0.0 101.9 jit_solution(3137143552502560276)
XLA Ops:
  0.6 0.1 pad_add_fusion.refs_0_.index_ref
  0.7 0.0 copy-start.2
  0.7 1.0 copy-done.2
  1.7 0.0 copy-start.3
  1.7 0.8 copy-done.3
  2.5 0.0 copy-start.10
  2.5 0.7 copy-done.10
  3.1 0.0 copy-start.11
  3.1 0.7 copy-done.11
  3.8 3.1 %restrict.1 = (f32[16,1024]{1,0:T(8,128)S(1)}, f32[8,16,256]{2,1,0:T(8,128)}, s32[1,64]{1,0:T(1,128)S(1)}) custom-call(s32[2]{0:T(128)S(1)} %pad_add_fusion.refs_0_.index_ref, s32[1,64]{1,0:T(1,128)S(1)} %copy-done.11, s32[1,192]{1,0:T(1,128)S(1)} %copy-done.10, f32[6,2,8192]{2,1,0:T(2,128)S(1)} %bitcast.11, s32[64,128]{1,0:T(8,128)S(1)} %bitcast.12), custom_call_target="tpu_custom_call" | custom-call | tf_op jit(solution)/shard_map/restrict/pallas_call | solution.py:387
  6.9 7.3 %all-to-all-start = ((f32[8,16,256]{2,1,0:T(8,128)}), f32[8,16,256]{2,1,0:T(8,128)S(1)}, u32[]{:S(2)}, u32[]{:S(2)}) async-start(f32[8,16,256]{2,1,0:T(8,128)} %get-tuple-element.27), calls=%async_computation | async-start | bytes 262144 | tf_op jit(solution)/shard_map/all_to_all | solution.py:392
  14.2 0.0 copy-start.5
  14.2 0.8 copy-done.5
  15.0 0.0 copy-start.6
  15.0 0.8 copy-done.6
  15.7 0.0 copy-start.7
  15.7 0.8 copy-done.7
  16.5 0.0 copy-start.9
  16.5 0.7 copy-done.9
  17.2 5.1 %prepare.1 = (bf16[1280,1024]{1,0:T(8,128)(2,1)S(1)}, bf16[1280,1024]{1,0:T(8,128)(2,1)S(1)}, f32[16,1024]{1,0:T(8,128)S(1)}, f32[16,1024]{1,0:T(8,128)S(1)}, f32[24,1024]{1,0:T(8,128)S(1)}) custom-call(s32[6,1024]{1,0:T(8,128)S(1)} %copy-done.5, f32[6,1024]{1,0:T(8,128)S(1)} %copy-done.6, f32[1,1024]{1,0:T(1,128)S(1)} %bitcast.14, f32[6,1024]{1,0:T(8,128)S(1)} %copy-done.7), custom_call_target="tpu_custom_call" | custom-call | tf_op jit(solution)/shard_map/prepare/pallas_call | solution.py:402
  22.3 0.0 copy-start
  22.3 1.5 %copy-done = bf16[1280,1024]{1,0:T(8,128)(2,1)} copy-done((bf16[1280,1024]{1,0:T(8,128)(2,1)}, bf16[1280,1024]{1,0:T(8,128)(2,1)S(1)}, u32[]{:S(2)}) %copy-start) | copy-done | bytes 2621464
  23.8 0.0 all-to-all-done.refs_1_
  23.8 0.7 arrive.1
  24.4 5.8 %all-gather = f32[64,1024]{1,0:T(8,128)S(1)} all-gather(f32[16,1024]{1,0:T(8,128)S(1)} %get-tuple-element.29), channel_id=2, replica_groups=mesh['cell'=8,'inst'=4] {'inst'}, dimensions={0}, use_global_device_ids=true | all-gather | bytes 327680 | tf_op jit(solution)/shard_map/all_gather | solution.py:398
  30.2 0.0 copy-start.1
  30.2 1.7 %copy-done.1 = bf16[1280,1024]{1,0:T(8,128)(2,1)S(1)} copy-done((bf16[1280,1024]{1,0:T(8,128)(2,1)S(1)}, bf16[1280,1024]{1,0:T(8,128)(2,1)}, u32[]{:S(2)}) %copy-start.1) | copy-done | bytes 2621464
  32.0 0.0 copy-start.8
  32.0 0.7 copy-done.8
  32.7 1.6 %begin.1 = (f32[16,1024]{1,0:T(8,128)S(1)}, f32[16,1024]{1,0:T(8,128)S(1)}, f32[8,56,256]{2,1,0:T(8,128)S(1)}) custom-call(s32[2]{0:T(128)S(1)} %pad_add_fusion.refs_0_.index_ref, f32[8,8]{1,0:T(8,128)S(1)} %copy-done.8, f32[4,16,1024]{2,1,0:T(8,128)S(1)} %bitcast.10, f32[16,1024]{1,0:T(8,128)S(1)} %get-tuple-element.30.inverse_ref.refs_4_, ...), custom_call_target="tpu_custom_call" | custom-call | tf_op jit(solution)/shard_map/begin/pallas_call | solution.py:405
  34.2 19.5 %all_to_all.20.refs_1_ = f32[8,56,256]{2,1,0:T(8,128)S(1)} all-to-all(f32[8,56,256]{2,1,0:T(8,128)S(1)} %get-tuple-element.36), channel_id=1, replica_groups=mesh['cell'=8,'inst'=4] {'cell'}, dimensions={0} | all-to-all | bytes 917504 | tf_op jit(solution)/shard_map/all_to_all | solution.py:410
  53.7 2.7 %double.3 = (f32[16,1024]{1,0:T(8,128)S(1)}, f32[8,32,256]{2,1,0:T(8,128)S(1)}, bf16[2,256,256]{2,1,0:T(8,128)(2,1)S(1)}, f32[16,256]{1,0:T(8,128)S(1)}) custom-call(s32[2]{0:T(128)S(1)} %pad_add_fusion.refs_0_.index_ref, f32[8,56,256]{2,1,0:T(8,128)S(1)} %all_to_all.20.refs_1_, f32[16,1024]{1,0:T(8,128)S(1)} %get-tuple-element.37.refs_2_, ...), custom_call_target="tpu_custom_call" | custom-call | tf_op jit(solution)/shard_map/double/pallas_call | solution.py:418
  56.4 12.3 %all_to_all.21.refs_1_ = f32[8,32,256]{2,1,0:T(8,128)S(1)} all-to-all(f32[8,32,256]{2,1,0:T(8,128)S(1)} %get-tuple-element.39), channel_id=1, replica_groups=mesh['cell'=8,'inst'=4] {'cell'}, dimensions={0} | all-to-all | bytes 524288 | tf_op jit(solution)/shard_map/all_to_all | solution.py:410
  68.7 2.5 %double.4 = (f32[16,1024]{1,0:T(8,128)S(1)}, f32[8,32,256]{2,1,0:T(8,128)S(1)}) custom-call(s32[2]{0:T(128)S(1)} %pad_add_fusion.refs_0_.index_ref, f32[8,32,256]{2,1,0:T(8,128)S(1)} %all_to_all.21.refs_1_, f32[16,1024]{1,0:T(8,128)S(1)} %get-tuple-element.40.refs_2_, f32[16,1024]{1,0:T(8,128)S(1)} %get-tuple-element.38.refs_3_, ...), custom_call_target="tpu_custom_call" | custom-call | tf_op jit(solution)/shard_map/double/pallas_call | solution.py:418
  71.2 12.0 %all_to_all.22.refs_1_ = f32[8,32,256]{2,1,0:T(8,128)S(1)} all-to-all(f32[8,32,256]{2,1,0:T(8,128)S(1)} %get-tuple-element.43), channel_id=1, replica_groups=mesh['cell'=8,'inst'=4] {'cell'}, dimensions={0} | all-to-all | bytes 524288 | tf_op jit(solution)/shard_map/all_to_all | solution.py:410
  83.2 0.0 copy-start.4
  83.2 1.7 %double.5 = (f32[16,1024]{1,0:T(8,128)S(1)}, f32[16,128]{1,0:T(8,128)S(1)}, f32[16,128]{1,0:T(8,128)S(1)}) custom-call(s32[2]{0:T(128)S(1)} %pad_add_fusion.refs_0_.index_ref, f32[8,32,256]{2,1,0:T(8,128)S(1)} %all_to_all.22.refs_1_, f32[16,1024]{1,0:T(8,128)S(1)} %get-tuple-element.44.refs_2_, f32[16,1024]{1,0:T(8,128)S(1)} %get-tuple-element.38.refs_3_, ...), custom_call_target="tpu_custom_call" | custom-call | tf_op jit(solution)/shard_map/double/pallas_call | solution.py:418
  84.9 2.3 %collective-permute-start = (f32[16,128]{1,0:T(8,128)S(1)}, f32[16,128]{1,0:T(8,128)S(1)}, u32[]{:S(2)}, u32[]{:S(2)}) collective-permute-start(f32[16,128]{1,0:T(8,128)S(1)} %get-tuple-element.46), channel_id=1, source_target_pairs={{0,28},{4,0},{8,4},{12,8},{16,12},{20,16},{24,20},{28,24},{1,29},{... | collective-permute-start | bytes 24584 | tf_op jit(solution)/shard_map/ppermute | solution.py:364
  87.2 0.0 collective-permute-start.1
  87.2 1.4 %collective-permute-done = f32[16,128]{1,0:T(8,128)S(1)} collective-permute-done((f32[16,128]{1,0:T(8,128)S(1)}, f32[16,128]{1,0:T(8,128)S(1)}, u32[]{:S(2)}, u32[]{:S(2)}) %collective-permute-start) | collective-permute-done | bytes 8224 | tf_op jit(solution)/shard_map/ppermute | solution.py:364
  88.6 5.0 %collective-permute-done.1 = f32[16,128]{1,0:T(8,128)S(1)} collective-permute-done((f32[16,128]{1,0:T(8,128)S(1)}, f32[16,128]{1,0:T(8,128)S(1)}, u32[]{:S(2)}, u32[]{:S(2)}) %collective-permute-start.1) | collective-permute-done | bytes 8224 | tf_op jit(solution)/shard_map/ppermute | solution.py:364
  93.6 6.1 %all-gather.1 = f32[64,1280]{1,0:T(8,128)S(1)} all-gather(f32[16,1280]{1,0:T(8,128)S(1)} %pad_maximum_fusion), channel_id=3, replica_groups=mesh['cell'=8,'inst'=4] {'inst'}, dimensions={0}, use_global_device_ids=true | all-gather | bytes 409600 | tf_op jit(solution)/shard_map/all_gather | solution.py:434
  99.6 0.0 copy-done.4
  99.6 2.2 %finish.1 = (f32[6,2,1024]{2,1,0:T(2,128)}, f32[6,2,8192]{2,1,0:T(2,128)}) custom-call(s32[2]{0:T(128)S(1)} %pad_add_fusion.refs_0_.index_ref, f32[8,8]{1,0:T(8,128)S(1)} %copy-done.8, s32[1,64]{1,0:T(1,128)S(1)} %get-tuple-element.26.order_ref, f32[4,16,1280]{2,1,0:T(8,128)S(1)} %bitcast.9, s32[64,128]{1,0:T(8,128)S(1)} %bitcast.13), custom_call_target="tpu_custom_call" | custom-call | tf_op jit(solution)/shard_map/finish/pallas_call | solution.py:435
  (1 shorter events, 0.0 us)
Async XLA Ops:
  0.7 1.0 copy-start.2
  1.7 0.8 copy-start.3
  2.5 0.7 copy-start.10
  3.1 0.7 copy-start.11
  6.9 16.9 %all-to-all-start = ((f32[8,16,256]{2,1,0:T(8,128)}), f32[8,16,256]{2,1,0:T(8,128)S(1)}, u32[]{:S(2)}, u32[]{:S(2)}) async-start(f32[8,16,256]{2,1,0:T(8,128)} %get-tuple-element.27), calls=%async_computation | async-start | bytes 262144 | tf_op jit(solution)/shard_map/all_to_all | solution.py:392
  14.2 0.8 copy-start.5
  15.0 0.8 copy-start.6
  15.7 0.8 copy-start.7
  16.5 0.7 copy-start.9
  22.3 1.5 %copy-start = (bf16[1280,1024]{1,0:T(8,128)(2,1)}, bf16[1280,1024]{1,0:T(8,128)(2,1)S(1)}, u32[]{:S(2)}) copy-start(bf16[1280,1024]{1,0:T(8,128)(2,1)S(1)} %get-tuple-element.35.low_ref.refs_7_) | copy-start | bytes 7864324
  30.2 1.7 %copy-start.1 = (bf16[1280,1024]{1,0:T(8,128)(2,1)S(1)}, bf16[1280,1024]{1,0:T(8,128)(2,1)}, u32[]{:S(2)}) copy-start(bf16[1280,1024]{1,0:T(8,128)(2,1)} %copy-done) | copy-start | bytes 7864324
  32.0 0.7 copy-start.8
  83.2 16.5 %copy-start.4 = (s32[8192]{0:T(1024)S(1)}, s32[8192]{0:T(1024)}, u32[]{:S(2)}) copy-start(s32[8192]{0:T(1024)} %param.10) | copy-start | bytes 98308
  84.9 3.7 %collective-permute-start = (f32[16,128]{1,0:T(8,128)S(1)}, f32[16,128]{1,0:T(8,128)S(1)}, u32[]{:S(2)}, u32[]{:S(2)}) collective-permute-start(f32[16,128]{1,0:T(8,128)S(1)} %get-tuple-element.46), channel_id=1, source_target_pairs={{0,28},{4,0},{8,4},{12,8},{16,12},{20,16},{24,20},{28,24},{1,29},{... | collective-permute-start | bytes 24584 | tf_op jit(solution)/shard_map/ppermute | solution.py:364
  87.2 6.3 %collective-permute-start.1 = (f32[16,128]{1,0:T(8,128)S(1)}, f32[16,128]{1,0:T(8,128)S(1)}, u32[]{:S(2)}, u32[]{:S(2)}) collective-permute-start(f32[16,128]{1,0:T(8,128)S(1)} %get-tuple-element.47), channel_id=1, source_target_pairs={{0,4},{4,8},{8,12},{12,16},{16,20},{20,24},{24,28},{28,0},{1,5},{5... | collective-permute-start | bytes 24584 | tf_op jit(solution)/shard_map/ppermute | solution.py:364

commit v3 on v2

--- a/solution.py
+++ b/solution.py
@@ -205,7 +205,7 @@
     return start_ref[...] + total * inverse_ref[...] - wave * coupled_ref[...] * swap_pairs(value)
 
 
-def begin_kernel(index_ref, basis_ref, gathered_ref, inverse_ref, coupled_ref, topology_ref, pack_ref, high_ref, low_ref,
+def begin_kernel(share, index_ref, basis_ref, gathered_ref, inverse_ref, coupled_ref, topology_ref, pack_ref, high_ref, low_ref,
                  start_ref, local_ref, send_ref):
     pair = index_ref[1]
     groups, height, coarse_dev = gathered_ref.shape
@@ -221,8 +221,38 @@
     local = local_part(start, start_ref, inverse_ref, coupled_ref, pair.astype(jnp.float32), high_ref, low_ref)
     local_ref[...] = local
     send = pack_halo(jnp.concatenate([start, local, topology_ref[...]], axis=0), pack_ref)
-    for target in range(send_ref.shape[0]):
-        send_ref[target] = send
+    taller = jnp.zeros((send_ref.shape[1] - height, send.shape[1]), jnp.float32)
+    everyone = jnp.concatenate([send[:height], taller], axis=0)
+    next_local = jnp.concatenate([send[height : 2 * height], taller], axis=0)
+    fill_send(send_ref, index_ref[0], share, everyone, (next_local, send[2 * height :]))
+
+
+def fill_send(send_ref, partition, share, everyone, for_one):
+    n_cell, height, width = send_ref.shape
+    halo = len(OFFSETS) * share
+    lane = lax.broadcasted_iota(jnp.int32, (height, width), 1)
+    for target in range(n_cell):
+        send_ref[target] = everyone
+    for slot, offset in enumerate(OFFSETS):
+        message = everyone
+        for place, part in enumerate(for_one):
+            begin = halo + place * share
+            inside = (lane >= begin) & (lane < begin + share)
+            message = jnp.where(inside, pltpu.roll(part, begin - slot * share, 1), message)
+        send_ref[lax.rem(partition - offset + n_cell, n_cell)] = message
+
+
+def told_of(partition, share, got_ref, place, height):
+    n_cell, _, width = got_ref.shape
+    lane = lax.broadcasted_iota(jnp.int32, (height, width), 1)
+    begin = (len(OFFSETS) + place) * share
+    told = jnp.zeros((height, width), jnp.float32)
+    for slot, offset in enumerate(OFFSETS):
+        sender = lax.rem(partition + offset + n_cell, n_cell)
+        inside = (lane >= slot * share) & (lane < (slot + 1) * share)
+        part = pltpu.roll(got_ref[sender, 0:height, :], width + slot * share - begin, 1)
+        told = jnp.where(inside, part, told)
+    return told
 
 
 def halo_of(partition, share, got_ref, top, height):
@@ -253,7 +283,7 @@
     out_refs = refs
     if first:
         out_refs, (edge_ref, halo_inverse_ref) = refs[:-2], refs[-2:]
-        told = halo_of(partition, share, got_ref, 2 * height, 24)
+        told = told_of(partition, share, got_ref, 1, 24)
         ids = told[:slots].astype(jnp.int32) - coarse_dev
         weights = told[8 : 8 + slots]
         rows = lax.broadcasted_iota(jnp.int32, (width, width), 0)
@@ -277,7 +307,7 @@
     for slot in range(len(OFFSETS)):
         inside = (lane >= slot * share) & (lane < (slot + 1) * share)
         edge_total = jnp.where(inside, spread[slot * height : (slot + 1) * height], edge_total)
-    next_halo = halo_of(partition, share, got_ref, height, height) + halo_inverse_ref[...] * edge_total
+    next_halo = told_of(partition, share, got_ref, 0, height) + halo_inverse_ref[...] * edge_total
     both = times(
         jnp.concatenate([halo_of(partition, share, got_ref, 0, height), next_halo], axis=0), halo_high, halo_low
     )
@@ -294,8 +324,7 @@
     local = local_part(value, start_ref, inverse_ref, coupled_ref, wave, high_ref, low_ref)
     out_ref[...] = local
     send = pack_halo(jnp.concatenate([value, local], axis=0), pack_ref)
-    for target in range(n_cell):
-        send_ref[target] = send
+    fill_send(send_ref, partition, share, send[:height], (send[height:],))
 
 
 def finish_kernel(index_ref, basis_ref, order_ref, gathered_ref, map_ref, coarse_ref, fine_ref, flat_ref):
@@ -376,8 +405,8 @@
     rows = inst_dev * var_count
     height = -(-(rows + 1) // 16) * 16
     halo = receive_lists.shape[1]
-    halo_pad = -(-halo // 256) * 256
     share = halo // (2 * RAD)
+    halo_pad = -(-(halo + 2 * share) // 256) * 256
     index = jnp.stack([lax.axis_index("cell"), lax.axis_index("inst")]).astype(jnp.int32)
     basis = jnp.asarray(fourier_basis())
     cell_map = fine_map.reshape(blocks, BLK)
@@ -403,14 +432,14 @@
         prepare_kernel, [half, half, state, state, f32(24, coarse_dev)], "prepare", (), 4
     )(neighbours, face_weights, spectral, diag_extra)
     start, local, send = call(
-        begin_kernel, [state, state, f32(n_cell, 2 * height + 24, halo_pad)], "begin", (0, 1), 9
+        lambda *refs: begin_kernel(share, *refs), [state, state, f32(n_cell, 24, halo_pad)], "begin", (0, 1), 9
     )(index, basis, gathered, inverse, coupled, topology, pack, high, low)
     edges = []
     for pair in range(ITERS // 2):
         got = lax.all_to_all(send, "cell", 0, 0)
         is_first = pair == 0
         is_last = pair == ITERS // 2 - 1
-        outs = [state, f32(n_cell, 2 * height, halo_pad)]
+        outs = [state, f32(n_cell, height, halo_pad)]
         if is_last:
             outs = [state, f32(height, LANES), f32(height, LANES)]
         if is_first:

time: 103 us -> 92.2 us (0.90)
  blocking collectives: 55.6 us -> 46.2 us
    all_to_all x3, blocking collectives: 43.8 us -> 34.3 us  [body(): got = lax.all_to_all(send, 'cell', 0, 0)]
  transfers between devices with their start and end apart: 3 -> 3, of which waited for: 2 -> 2; matrix products, arithmetic and copies ran while one was open for 0% -> 0% of each run, Pallas kernels for 5% -> 6%
where the time goes in v3:
time: 92.2 us; the launch traced here: 91.4 us
  blocking collectives  46.2 us (50%)
  Pallas kernels  19.8 us (21%)
  local copies, waits for them, and re-layouts  9.96 us (11%)
  starting transfers between devices  9.37 us (10%)
  waiting for transfers between devices  5.4 us (6%)
    all_to_all x3, blocking collectives, body(): got = lax.all_to_all(send, 'cell', 0, 0)  34.3 us
    unnamed x24, local copies, waits for them, and re-layouts  9.96 us
    all_to_all x1, starting transfers between devices, body(): got = lax.all_to_all(send, 'cell', 0, 0)  7.32 us
    pallas_call x3, Pallas kernels, body(): call(lambda *refs: double_kernel(share, is_first, is_last, slots, var_cou...  7.05 us
    all_gather x1, blocking collectives, body(): gathered = lax.all_gather(joined, 'inst', axis=0)  6.09 us
    all_gather x1, blocking collectives, body(): gathered = lax.all_gather(arrived, 'inst', axis=0)  5.78 us
    ppermute x2, waiting for transfers between devices, shifted(): return lax.ppermute(value, axis, pairs)  5.39 us
    pallas_call x1, Pallas kernels, body(): call(prepare_kernel, [half, half, state, state, f32(24, coarse_dev)], 'pr...  5.1 us
  transfers between devices with their start and end apart: 3, of which 2 were waited for; matrix products, arithmetic and copies ran while one was open for 0% of the time, Pallas kernels for 6%

profile of v3, /device:TPU:0, one launch (start us, length us, event | category | flops | bytes accessed | tf_op | source)
XLA Modules:
  0.0 91.4 jit_solution(10689674992030617052)
XLA Ops:
  0.6 0.1 pad_add_fusion.refs_0_.index_ref
  0.7 0.0 copy-start.2
  0.7 1.0 %copy-done.2 = f32[2,6,8192]{2,0,1:T(2,128)S(1)} copy-done((f32[2,6,8192]{2,0,1:T(2,128)S(1)}, f32[2,6,8192]{2,0,1:T(2,128)}, u32[]{:S(2)}) %copy-start.2) | copy-done | bytes 393240
  1.7 0.0 copy-start.3
  1.7 0.8 copy-done.3
  2.5 0.0 copy-start.10
  2.5 0.7 copy-done.10
  3.1 0.0 copy-start.11
  3.1 0.7 copy-done.11
  3.8 3.1 %restrict.1 = (f32[16,1024]{1,0:T(8,128)S(1)}, f32[8,16,256]{2,1,0:T(8,128)}, s32[1,64]{1,0:T(1,128)S(1)}) custom-call(s32[2]{0:T(128)S(1)} %pad_add_fusion.refs_0_.index_ref, s32[1,64]{1,0:T(1,128)S(1)} %copy-done.11, s32[1,192]{1,0:T(1,128)S(1)} %copy-done.10, f32[6,2,8192]{2,1,0:T(2,128)S(1)} %bitcast.11, s32[64,128]{1,0:T(8,128)S(1)} %bitcast.12), custom_call_target="tpu_custom_call" | custom-call | tf_op jit(solution)/shard_map/restrict/pallas_call | solution.py:416
  6.9 7.3 %all-to-all-start = ((f32[8,16,256]{2,1,0:T(8,128)}), f32[8,16,256]{2,1,0:T(8,128)S(1)}, u32[]{:S(2)}, u32[]{:S(2)}) async-start(f32[8,16,256]{2,1,0:T(8,128)} %get-tuple-element.27), calls=%async_computation | async-start | bytes 262144 | tf_op jit(solution)/shard_map/all_to_all | solution.py:421
  14.2 0.0 copy-start.5
  14.2 0.8 copy-done.5
  15.0 0.0 copy-start.6
  15.0 0.8 copy-done.6
  15.7 0.0 copy-start.7
  15.7 0.8 copy-done.7
  16.5 0.0 copy-start.9
  16.5 0.7 copy-done.9
  17.2 5.1 %prepare.1 = (bf16[1280,1024]{1,0:T(8,128)(2,1)S(1)}, bf16[1280,1024]{1,0:T(8,128)(2,1)S(1)}, f32[16,1024]{1,0:T(8,128)S(1)}, f32[16,1024]{1,0:T(8,128)S(1)}, f32[24,1024]{1,0:T(8,128)S(1)}) custom-call(s32[6,1024]{1,0:T(8,128)S(1)} %copy-done.5, f32[6,1024]{1,0:T(8,128)S(1)} %copy-done.6, f32[1,1024]{1,0:T(1,128)S(1)} %bitcast.14, f32[6,1024]{1,0:T(8,128)S(1)} %copy-done.7), custom_call_target="tpu_custom_call" | custom-call | tf_op jit(solution)/shard_map/prepare/pallas_call | solution.py:431
  22.3 0.0 copy-start
  22.3 1.5 %copy-done = bf16[1280,1024]{1,0:T(8,128)(2,1)} copy-done((bf16[1280,1024]{1,0:T(8,128)(2,1)}, bf16[1280,1024]{1,0:T(8,128)(2,1)S(1)}, u32[]{:S(2)}) %copy-start) | copy-done | bytes 2621464
  23.8 0.0 all-to-all-done.refs_1_
  23.8 0.7 arrive.1
  24.4 5.8 %all-gather = f32[64,1024]{1,0:T(8,128)S(1)} all-gather(f32[16,1024]{1,0:T(8,128)S(1)} %get-tuple-element.29), channel_id=2, replica_groups=mesh['cell'=8,'inst'=4] {'inst'}, dimensions={0}, use_global_device_ids=true | all-gather | bytes 327680 | tf_op jit(solution)/shard_map/all_gather | solution.py:427
  30.2 0.0 copy-start.1
  30.2 1.7 %copy-done.1 = bf16[1280,1024]{1,0:T(8,128)(2,1)S(1)} copy-done((bf16[1280,1024]{1,0:T(8,128)(2,1)S(1)}, bf16[1280,1024]{1,0:T(8,128)(2,1)}, u32[]{:S(2)}) %copy-start.1) | copy-done | bytes 2621464
  32.0 0.0 copy-start.8
  32.0 0.7 copy-done.8
  32.7 1.7 %begin.1 = (f32[16,1024]{1,0:T(8,128)S(1)}, f32[16,1024]{1,0:T(8,128)S(1)}, f32[8,24,256]{2,1,0:T(8,128)S(1)}) custom-call(s32[2]{0:T(128)S(1)} %pad_add_fusion.refs_0_.index_ref, f32[8,8]{1,0:T(8,128)S(1)} %copy-done.8, f32[4,16,1024]{2,1,0:T(8,128)S(1)} %bitcast.10, f32[16,1024]{1,0:T(8,128)S(1)} %get-tuple-element.30.refs_3_.refs_4_, ...), custom_call_target="tpu_custom_call" | custom-call | tf_op jit(solution)/shard_map/begin/pallas_call | solution.py:434
  34.3 14.3 %all_to_all.20.refs_1_ = f32[8,24,256]{2,1,0:T(8,128)S(1)} all-to-all(f32[8,24,256]{2,1,0:T(8,128)S(1)} %get-tuple-element.36), channel_id=1, replica_groups=mesh['cell'=8,'inst'=4] {'cell'}, dimensions={0} | all-to-all | bytes 393216 | tf_op jit(solution)/shard_map/all_to_all | solution.py:439
  48.6 2.8 %double.3 = (f32[16,1024]{1,0:T(8,128)S(1)}, f32[8,16,256]{2,1,0:T(8,128)S(1)}, bf16[2,256,256]{2,1,0:T(8,128)(2,1)S(1)}, f32[16,256]{1,0:T(8,128)S(1)}) custom-call(s32[2]{0:T(128)S(1)} %pad_add_fusion.refs_0_.index_ref, f32[8,24,256]{2,1,0:T(8,128)S(1)} %all_to_all.20.refs_1_, f32[16,1024]{1,0:T(8,128)S(1)} %get-tuple-element.37.refs_2_, ...), custom_call_target="tpu_custom_call" | custom-call | tf_op jit(solution)/shard_map/double/pallas_call | solution.py:447
  51.4 10.3 %all_to_all.21.refs_1_ = f32[8,16,256]{2,1,0:T(8,128)S(1)} all-to-all(f32[8,16,256]{2,1,0:T(8,128)S(1)} %get-tuple-element.39), channel_id=1, replica_groups=mesh['cell'=8,'inst'=4] {'cell'}, dimensions={0} | all-to-all | bytes 262144 | tf_op jit(solution)/shard_map/all_to_all | solution.py:439
  61.7 2.6 %double.4 = (f32[16,1024]{1,0:T(8,128)S(1)}, f32[8,16,256]{2,1,0:T(8,128)S(1)}) custom-call(s32[2]{0:T(128)S(1)} %pad_add_fusion.refs_0_.index_ref, f32[8,16,256]{2,1,0:T(8,128)S(1)} %all_to_all.21.refs_1_, f32[16,1024]{1,0:T(8,128)S(1)} %get-tuple-element.40.refs_2_, f32[16,1024]{1,0:T(8,128)S(1)} %get-tuple-element.38.refs_3_, ...), custom_call_target="tpu_custom_call" | custom-call | tf_op jit(solution)/shard_map/double/pallas_call | solution.py:447
  64.2 9.7 %all_to_all.22.refs_1_ = f32[8,16,256]{2,1,0:T(8,128)S(1)} all-to-all(f32[8,16,256]{2,1,0:T(8,128)S(1)} %get-tuple-element.43), channel_id=1, replica_groups=mesh['cell'=8,'inst'=4] {'cell'}, dimensions={0} | all-to-all | bytes 262144 | tf_op jit(solution)/shard_map/all_to_all | solution.py:439
  74.0 0.0 copy-start.4
  74.0 1.7 %double.5 = (f32[16,1024]{1,0:T(8,128)S(1)}, f32[16,128]{1,0:T(8,128)S(1)}, f32[16,128]{1,0:T(8,128)S(1)}) custom-call(s32[2]{0:T(128)S(1)} %pad_add_fusion.refs_0_.index_ref, f32[8,16,256]{2,1,0:T(8,128)S(1)} %all_to_all.22.refs_1_, f32[16,1024]{1,0:T(8,128)S(1)} %get-tuple-element.44.refs_2_, f32[16,1024]{1,0:T(8,128)S(1)} %get-tuple-element.38.refs_3_, ...), custom_call_target="tpu_custom_call" | custom-call | tf_op jit(solution)/shard_map/double/pallas_call | solution.py:447
  75.7 1.1 %collective-permute-start = (f32[16,128]{1,0:T(8,128)S(1)}, f32[16,128]{1,0:T(8,128)S(1)}, u32[]{:S(2)}, u32[]{:S(2)}) collective-permute-start(f32[16,128]{1,0:T(8,128)S(1)} %get-tuple-element.46), channel_id=1, source_target_pairs={{0,28},{4,0},{8,4},{12,8},{16,12},{20,16},{24,20},{28,24},{1,29},{... | collective-permute-start | bytes 24584 | tf_op jit(solution)/shard_map/ppermute | solution.py:393
  76.8 1.0 %collective-permute-start.1 = (f32[16,128]{1,0:T(8,128)S(1)}, f32[16,128]{1,0:T(8,128)S(1)}, u32[]{:S(2)}, u32[]{:S(2)}) collective-permute-start(f32[16,128]{1,0:T(8,128)S(1)} %get-tuple-element.47), channel_id=1, source_target_pairs={{0,4},{4,8},{8,12},{12,16},{16,20},{20,24},{24,28},{28,0},{1,5},{5... | collective-permute-start | bytes 24584 | tf_op jit(solution)/shard_map/ppermute | solution.py:393
  77.7 1.6 %collective-permute-done = f32[16,128]{1,0:T(8,128)S(1)} collective-permute-done((f32[16,128]{1,0:T(8,128)S(1)}, f32[16,128]{1,0:T(8,128)S(1)}, u32[]{:S(2)}, u32[]{:S(2)}) %collective-permute-start) | collective-permute-done | bytes 8224 | tf_op jit(solution)/shard_map/ppermute | solution.py:393
  79.3 3.8 %collective-permute-done.1 = f32[16,128]{1,0:T(8,128)S(1)} collective-permute-done((f32[16,128]{1,0:T(8,128)S(1)}, f32[16,128]{1,0:T(8,128)S(1)}, u32[]{:S(2)}, u32[]{:S(2)}) %collective-permute-start.1) | collective-permute-done | bytes 8224 | tf_op jit(solution)/shard_map/ppermute | solution.py:393
  83.1 6.1 %all-gather.1 = f32[64,1280]{1,0:T(8,128)S(1)} all-gather(f32[16,1280]{1,0:T(8,128)S(1)} %pad_maximum_fusion), channel_id=3, replica_groups=mesh['cell'=8,'inst'=4] {'inst'}, dimensions={0}, use_global_device_ids=true | all-gather | bytes 409600 | tf_op jit(solution)/shard_map/all_gather | solution.py:463
  89.2 0.0 copy-done.4
  89.2 2.2 %finish.1 = (f32[6,2,1024]{2,1,0:T(2,128)}, f32[6,2,8192]{2,1,0:T(2,128)}) custom-call(s32[2]{0:T(128)S(1)} %pad_add_fusion.refs_0_.index_ref, f32[8,8]{1,0:T(8,128)S(1)} %copy-done.8, s32[1,64]{1,0:T(1,128)S(1)} %get-tuple-element.26.order_ref, f32[4,16,1280]{2,1,0:T(8,128)S(1)} %bitcast.9, s32[64,128]{1,0:T(8,128)S(1)} %bitcast.13), custom_call_target="tpu_custom_call" | custom-call | tf_op jit(solution)/shard_map/finish/pallas_call | solution.py:464
  (1 shorter events, 0.0 us)
Async XLA Ops:
  0.7 1.0 %copy-start.2 = (f32[2,6,8192]{2,0,1:T(2,128)S(1)}, f32[2,6,8192]{2,0,1:T(2,128)}, u32[]{:S(2)}) copy-start(f32[2,6,8192]{2,0,1:T(2,128)} %param.9) | copy-start | bytes 1179652
  1.7 0.8 copy-start.3
  2.5 0.7 copy-start.10
  3.1 0.7 copy-start.11
  6.9 16.9 %all-to-all-start = ((f32[8,16,256]{2,1,0:T(8,128)}), f32[8,16,256]{2,1,0:T(8,128)S(1)}, u32[]{:S(2)}, u32[]{:S(2)}) async-start(f32[8,16,256]{2,1,0:T(8,128)} %get-tuple-element.27), calls=%async_computation | async-start | bytes 262144 | tf_op jit(solution)/shard_map/all_to_all | solution.py:421
  14.2 0.8 copy-start.5
  15.0 0.8 copy-start.6
  15.7 0.8 copy-start.7
  16.5 0.7 copy-start.9
  22.3 1.5 %copy-start = (bf16[1280,1024]{1,0:T(8,128)(2,1)}, bf16[1280,1024]{1,0:T(8,128)(2,1)S(1)}, u32[]{:S(2)}) copy-start(bf16[1280,1024]{1,0:T(8,128)(2,1)S(1)} %get-tuple-element.35.refs_8_.refs_7_) | copy-start | bytes 7864324
  30.2 1.7 %copy-start.1 = (bf16[1280,1024]{1,0:T(8,128)(2,1)S(1)}, bf16[1280,1024]{1,0:T(8,128)(2,1)}, u32[]{:S(2)}) copy-start(bf16[1280,1024]{1,0:T(8,128)(2,1)} %copy-done) | copy-start | bytes 7864324
  32.0 0.7 copy-start.8
  74.0 15.2 %copy-start.4 = (s32[8192]{0:T(1024)S(1)}, s32[8192]{0:T(1024)}, u32[]{:S(2)}) copy-start(s32[8192]{0:T(1024)} %param.10) | copy-start | bytes 98308
  75.7 3.7 %collective-permute-start = (f32[16,128]{1,0:T(8,128)S(1)}, f32[16,128]{1,0:T(8,128)S(1)}, u32[]{:S(2)}, u32[]{:S(2)}) collective-permute-start(f32[16,128]{1,0:T(8,128)S(1)} %get-tuple-element.46), channel_id=1, source_target_pairs={{0,28},{4,0},{8,4},{12,8},{16,12},{20,16},{24,20},{28,24},{1,29},{... | collective-permute-start | bytes 24584 | tf_op jit(solution)/shard_map/ppermute | solution.py:393
  76.8 6.3 %collective-permute-start.1 = (f32[16,128]{1,0:T(8,128)S(1)}, f32[16,128]{1,0:T(8,128)S(1)}, u32[]{:S(2)}, u32[]{:S(2)}) collective-permute-start(f32[16,128]{1,0:T(8,128)S(1)} %get-tuple-element.47), channel_id=1, source_target_pairs={{0,4},{4,8},{8,12},{12,16},{16,20},{20,24},{24,28},{28,0},{1,5},{5... | collective-permute-start | bytes 24584 | tf_op jit(solution)/shard_map/ppermute | solution.py:393
